TPU v7x, 32 devices: a whole 2x2x4 slice. The times are simulated.
32 devices in a mesh: head: 4 (over z), pts: 8 (over y, x, core).
Axes of the slice: x: 2, y: 2, z: 4, core: 2. Of those that a mesh axis runs over, the one named last changes fastest.
Arguments:
- layer_inputs_trainorder: bfloat16 [196608, 256], P(('head', 'pts')), may hold values from -6 to 6
- inference_placement: int32 [196608], P(('head', 'pts')), may hold values from 0 to 196607, as said below
- initial_layernorm_gain: float32 [256], replicated, may hold values from 0.1 to 1.9
- initial_layernorm_offset: float32 [256], replicated, may hold values from -2 to 2
- attribute_projection: bfloat16 [256, 256], replicated, may hold values from -0.375 to 0.375
- assignment_feeder_projection: bfloat16 [256, 256], replicated, may hold values from -0.375 to 0.375
- partition_projection: bfloat16 [16, 32], replicated, may hold values from -1.5 to 1.5
- partition_offset: float32 [32], replicated, may hold values from -4 to 4
- softmax_sharpness: float32 [16], P('head'), may hold values from 0.03 to 1
- partition_question_map: float32 [16, 16], replicated, may hold values from -1.5 to 1.5
- partition_lookup_map: float32 [16, 16], replicated, may hold values from -1.5 to 1.5
- partition_content_map: float32 [16, 16], replicated, may hold values from -1.5 to 1.5
- emitted_projection: bfloat16 [256, 256], replicated, may hold values from -0.375 to 0.375
- emitted_offset: float32 [256], replicated, may hold values from -2 to 2
- latter_layernorm_gain: float32 [256], replicated, may hold values from 0.1 to 1.9
- latter_layernorm_offset: float32 [256], replicated, may hold values from -2 to 2
- perceptron_entry_map: bfloat16 [256, 1024], replicated, may hold values from -0.375 to 0.375
- perceptron_entry_offset: float32 [1024], replicated, may hold values from -2 to 2
- perceptron_exit_map: bfloat16 [1024, 256], replicated, may hold values from -0.1875 to 0.1875
- perceptron_exit_offset: float32 [256], replicated, may hold values from -2 to 2
Outputs:
- served: bfloat16 [8, 24576, 256], P('pts', 'head')
Inputs may be any that keep to these rules, and one draw needn't show every extreme that they name: inference_placement is a permutation of all points; of the 6144 points of each aligned block of the training order, exactly 192 go to each aligned block of 6144 serving positions.
All inputs are finite; a program needn't handle non-finite values.
Results may differ from a plain program's by a relative error of at most 0.0035.
The roundings to bfloat16 on the way count: a program that leaves them out, or rounds other values in their place, can miss the bound.
Values may be sent and summed in bfloat16 or wider, within the bound.
No kernel may reach another device: no remote copies, remote signals or barrier semaphores. Data moves between devices by JAX's collectives and lax.ppermute only.
A program may use at most 128 MiB of HBM per device.

v0:
```python
import functools
import math

import jax
import jax.numpy as jnp
from jax import lax
from jax.experimental import pallas as pl
from jax.experimental.pallas import tpu as pltpu
from jax.sharding import PartitionSpec as P


F32 = jnp.float32
BF16 = jnp.bfloat16
LANES = 128
TAIL = 8
BLOCK = 1024
EPS_NORM = 1e-05
LOG2E = math.log2(math.e)
NT = (((1,), (1,)), ((), ()))
TN = (((0,), (0,)), ((), ()))
NN = (((1,), (0,)), ((), ()))
VMEM = 56 * 1024 * 1024


def whole(shape):
    return pl.BlockSpec(shape, lambda *_: (0,) * len(shape))


def params():
    return pltpu.CompilerParams(vmem_limit_bytes=VMEM)


def floor_div(value, divisor):
    return jnp.floor((value + 0.5) * (1.0 / divisor))


def norm_rows(row_block, gain, bias):
    mean = jnp.mean(row_block, axis=-1, keepdims=True)
    centred = row_block - mean
    spread = jnp.mean(centred * centred, axis=-1, keepdims=True)
    return centred * lax.rsqrt(spread + EPS_NORM) * gain + bias


def rank_kernel(place_ref, list_ref, tail_ref, hot_ref, count_ref, key_ref, *, local, groups, shards):
    devices = groups * shards
    chunks = place_ref.shape[0]
    padded = list_ref.shape[1]
    placement = place_ref[...].astype(F32)
    block = floor_div(placement, local)
    within = placement - block * local
    outer = floor_div(block, groups)
    target = (block - outer * groups) * shards + outer
    high = floor_div(within, LANES)
    low = within - high * LANES
    ids = lax.broadcasted_iota(jnp.int32, (devices, LANES), 0).astype(F32)
    for c in range(chunks):
        hot = (ids == target[c : c + 1, :]).astype(F32)
        hot_ref[:, c * LANES : (c + 1) * LANES] = hot.astype(BF16)
    before = lax.broadcasted_iota(jnp.int32, (LANES, LANES), 0) < lax.broadcasted_iota(
        jnp.int32, (LANES, LANES), 1
    )
    prefix = jnp.concatenate(
        [before.astype(F32), jnp.ones((LANES, LANES), F32)], axis=1
    ).astype(BF16)
    for c in range(chunks):
        count_ref[c * devices : (c + 1) * devices, :] = jnp.dot(
            hot_ref[:, c * LANES : (c + 1) * LANES], prefix, preferred_element_type=F32
        )
    carry = jnp.zeros((devices, LANES), F32)
    slots = lax.broadcasted_iota(jnp.int32, (padded, LANES), 0).astype(F32)
    lane = lax.broadcasted_iota(jnp.int32, (1, LANES), 1).astype(F32)
    for c in range(chunks):
        counts = count_ref[c * devices : (c + 1) * devices, :]
        hot = hot_ref[:, c * LANES : (c + 1) * LANES].astype(F32)
        rank = jnp.sum(hot * (counts[:, :LANES] + carry), axis=0, keepdims=True)
        carry = carry + counts[:, LANES:]
        chosen = slots == rank
        values = (high[c : c + 1, :], low[c : c + 1, :], float(c), lane)
        for k, value in enumerate(values):
            key_ref[k * padded : (k + 1) * padded, c * LANES : (c + 1) * LANES] = jnp.where(
                chosen, value, 0.0
            ).astype(BF16)
    codes = lax.dot_general(hot_ref[...], key_ref[...], NT, preferred_element_type=F32)
    tail_ref[...] = jnp.zeros_like(tail_ref)
    tail_ref[:devices, :padded] = codes[:, :padded]
    tail_ref[devices:, :padded] = codes[:, padded : 2 * padded]
    source = codes[:, 2 * padded : 3 * padded] * LANES + codes[:, 3 * padded :]
    list_ref[...] = source.astype(jnp.int32)


def rank_rows(placement, local, width, groups, shards):
    devices = groups * shards
    per = local // devices
    padded = -(-per // LANES) * LANES
    chunks = local // LANES
    return pl.pallas_call(
        functools.partial(rank_kernel, local=local, groups=groups, shards=shards),
        out_shape=(
            jax.ShapeDtypeStruct((devices, padded), jnp.int32),
            jax.ShapeDtypeStruct((2 * devices, width), F32),
        ),
        scratch_shapes=[
            pltpu.VMEM((devices, local), BF16),
            pltpu.VMEM((chunks * devices, 2 * LANES), F32),
            pltpu.VMEM((4 * padded, local), BF16),
        ],
        compiler_params=params(),
        name="rank_rows",
    )(placement.reshape(chunks, LANES))


def gather_kernel(list_ref, x_ref, *refs, start, counts, tailed):
    tail_ref = refs[0] if tailed else None
    outs = refs[1 if tailed else 0 : -2]
    src, dst = refs[-2:]
    local, width = x_ref.shape
    devices = list_ref.shape[0]
    total = sum(counts)

    def widen(c, carry):
        row = pl.multiple_of(c * LANES, LANES)
        src[pl.ds(row, LANES), :] = x_ref[pl.ds(row, LANES), :LANES].astype(F32)
        src[pl.ds(row + local, LANES), :] = x_ref[pl.ds(row, LANES), LANES:].astype(F32)
        return carry

    lax.fori_loop(0, local // LANES, widen, 0)
    line = lax.broadcasted_iota(jnp.int32, (TAIL, width), 0)

    def fetch(d, carry):
        for j in range(total):
            row = list_ref[d, start + j]
            dst[j : j + 1, :] = src[pl.ds(row, 1), :]
            dst[total + j : total + j + 1, :] = src[pl.ds(row + local, 1), :]
        done = 0
        for out, count in zip(outs, counts):
            out[d, :count, :LANES] = dst[done : done + count, :].astype(BF16)
            out[d, :count, LANES:] = dst[total + done : total + done + count, :].astype(BF16)
            done += count
        if tailed:
            high = tail_ref[pl.ds(d, 1), :]
            low = tail_ref[pl.ds(d + devices, 1), :]
            codes = jnp.where(line == 0, high, jnp.where(line == 1, low, 0.0))
            outs[0][d, counts[0] :, :] = codes.astype(BF16)
        return carry

    lax.fori_loop(0, devices, fetch, 0)


def gather_rows(lists, rows, tail, start, counts):
    local, width = rows.shape
    devices = lists.shape[0]
    tailed = tail is not None
    vmem = pl.BlockSpec(memory_space=pltpu.VMEM)
    out_shape = [
        jax.ShapeDtypeStruct((devices, n + (TAIL if tailed else 0), width), BF16) for n in counts
    ]
    return pl.pallas_call(
        functools.partial(gather_kernel, start=start, counts=counts, tailed=tailed),
        in_specs=[pl.BlockSpec(memory_space=pltpu.SMEM), vmem, *([vmem] if tailed else [])],
        out_shape=out_shape,
        scratch_shapes=[
            pltpu.VMEM((2 * local, LANES), F32),
            pltpu.VMEM((2 * sum(counts), LANES), F32),
        ],
        compiler_params=params(),
        cost_estimate=pl.CostEstimate(
            flops=2_000_000 * devices * sum(counts), bytes_accessed=6_000_000, transcendentals=0
        ),
        name="gather_first" if tailed else "gather_rest",
    )(lists, rows, *([tail] if tailed else []))


def slice_weights(standard, feeder_t, logit_t, sharp_ref, offset_ref, logit_ref, weight_ref, total_ref):
    heads = sharp_ref.shape[0]
    slices = offset_ref.shape[1]
    middle = lax.dot_general(feeder_t[...], standard, NT, preferred_element_type=F32).astype(BF16)
    logit_ref[...] = jnp.dot(logit_t[...], middle, preferred_element_type=F32)
    sharp = jnp.broadcast_to(sharp_ref[...], (heads, LANES))
    for start in range(0, weight_ref.shape[1], LANES):
        lanes = pl.ds(start, LANES)
        top = None
        for m in range(slices):
            value = (logit_ref[m * heads : (m + 1) * heads, lanes] + offset_ref[0, m]) * sharp
            top = value if top is None else jnp.maximum(top, value)
        total = None
        for m in range(slices):
            value = (logit_ref[m * heads : (m + 1) * heads, lanes] + offset_ref[0, m]) * sharp
            value = jnp.exp2(value - top)
            logit_ref[m * heads : (m + 1) * heads, lanes] = value
            total = value if total is None else total + value
        scale = 1.0 / total
        for m in range(slices):
            value = logit_ref[m * heads : (m + 1) * heads, lanes] * scale
            weight_ref[m * heads : (m + 1) * heads, lanes] = value.astype(BF16)
            if total_ref is not None:
                total_ref[m * heads : (m + 1) * heads, :] += value


def head_mask(rows, width, heads):
    row_head = lax.broadcasted_iota(jnp.int32, (rows, width), 0) % heads
    return row_head == lax.broadcasted_iota(jnp.int32, (rows, width), 1) // (width // heads)


def repeat_heads(value, width, dims):
    feature = value.shape[dims[0][0][0]]
    pick = lax.broadcasted_iota(jnp.int32, (feature, width), 1) % feature == lax.broadcasted_iota(
        jnp.int32, (feature, width), 0
    )
    return lax.dot_general(
        value, pick.astype(F32), dims, precision=lax.Precision.HIGHEST, preferred_element_type=F32
    )


def sums_kernel(
    x_ref, gain, bias, attribute, feeder_t, partition, sharp_ref, offset_ref,
    packed_ref, logit_t, logit_ref, weight_ref, total_ref, numer_ref,
):
    step = pl.program_id(0)
    heads = sharp_ref.shape[0]
    rows, width = numer_ref.shape
    slices = rows // heads

    @pl.when(step == 0)
    def _():
        total_ref[...] = jnp.zeros_like(total_ref)
        numer_ref[...] = jnp.zeros_like(numer_ref)
        wide = repeat_heads(partition[...].astype(F32), width, TN)
        wide = jnp.broadcast_to(wide[:, None, :], (slices, heads, width))
        logit_t[...] = jnp.where(
            head_mask(rows, width, heads), wide.reshape(rows, width), 0.0
        ).astype(BF16)

    standard = norm_rows(x_ref[...].astype(F32), gain[...], bias[...]).astype(BF16)
    features = jnp.dot(standard, attribute[...], preferred_element_type=F32).astype(BF16)
    slice_weights(
        standard, feeder_t, logit_t, sharp_ref, offset_ref, logit_ref, weight_ref, total_ref
    )
    numer_ref[...] += jnp.dot(weight_ref[...], features, preferred_element_type=F32)

    @pl.when(step == pl.num_programs(0) - 1)
    def _():
        own = jnp.where(head_mask(rows, width, heads), numer_ref[...], 0.0)
        packed_ref[:, :width] = jnp.sum(own.reshape(slices, heads, width), axis=1)
        sums = jnp.sum(total_ref[...], axis=1, keepdims=True)
        lane = lax.broadcasted_iota(jnp.int32, (rows, LANES), 1)
        row_head = lax.broadcasted_iota(jnp.int32, (rows, LANES), 0) % heads
        own = jnp.where(row_head == lane, sums, 0.0)
        packed_ref[:, width:] = jnp.sum(own.reshape(slices, heads, LANES), axis=1)


def local_sums(x, gain, bias, attribute, feeder_t, partition, sharp, offset, block):
    local, width = x.shape
    heads = sharp.shape[0]
    slices = partition.shape[1]
    rows = slices * heads
    return pl.pallas_call(
        sums_kernel,
        grid=(local // block,),
        in_specs=[
            pl.BlockSpec((block, width), lambda i: (i, 0)),
            whole(gain.shape), whole(bias.shape), whole(attribute.shape), whole(feeder_t.shape),
            whole(partition.shape), whole(sharp.shape),
            pl.BlockSpec(memory_space=pltpu.SMEM),
        ],
        out_specs=(whole((slices, width + LANES)), whole((rows, width))),
        out_shape=(
            jax.ShapeDtypeStruct((slices, width + LANES), F32),
            jax.ShapeDtypeStruct((rows, width), BF16),
        ),
        scratch_shapes=[
            pltpu.VMEM((rows, block), F32),
            pltpu.VMEM((rows, block), BF16),
            pltpu.VMEM((rows, LANES), F32),
            pltpu.VMEM((rows, width), F32),
        ],
        compiler_params=params(),
        cost_estimate=pl.CostEstimate(flops=5_000_000_000, bytes_accessed=4_000_000, transcendentals=3_000_000),
        name="local_sums",
    )(x, gain, bias, attribute, feeder_t, partition, sharp, offset)


def attention_kernel(packed_ref, question, lookup, content, mix_t, *, heads):
    highest = lax.Precision.HIGHEST
    slices = packed_ref.shape[0]
    width = packed_ref.shape[1] - LANES
    feature = width // heads
    rows = slices * heads
    spread = (
        lax.broadcasted_iota(jnp.int32, (LANES, width), 0)
        == lax.broadcasted_iota(jnp.int32, (LANES, width), 1) // feature
    ).astype(F32)
    totals = jnp.dot(packed_ref[:, width:], spread, precision=highest, preferred_element_type=F32)
    token = packed_ref[:, :width] / (totals + 1e-05)
    own = (
        lax.broadcasted_iota(jnp.int32, (width, width), 0) // feature
        == lax.broadcasted_iota(jnp.int32, (width, width), 1) // feature
    )

    def per_head(weight):
        wide = repeat_heads(weight[...], width, NN)
        tiled = jnp.broadcast_to(wide[None], (heads, feature, width)).reshape(width, width)
        return jnp.dot(token, jnp.where(own, tiled, 0.0), precision=highest, preferred_element_type=F32)

    query = per_head(question)
    key = per_head(lookup)
    value = per_head(content)
    mask = head_mask(rows, width, heads)
    query = jnp.broadcast_to(query[:, None, :], (slices, heads, width)).reshape(rows, width)
    query = jnp.where(mask, query, 0.0)
    scores = lax.dot_general(query, key, NT, precision=highest, preferred_element_type=F32)
    scores = scores * (1.0 / math.sqrt(feature))
    scores = jnp.exp(scores - jnp.max(scores, axis=-1, keepdims=True))
    attention = scores / jnp.sum(scores, axis=-1, keepdims=True)
    mixed = jnp.dot(attention, value, precision=highest, preferred_element_type=F32)
    mix_t[...] = jnp.where(mask, mixed, 0.0).T.astype(BF16)


def slice_attention(packed, question, lookup, content, heads):
    slices = packed.shape[0]
    width = packed.shape[1] - LANES
    return pl.pallas_call(
        functools.partial(attention_kernel, heads=heads),
        out_shape=jax.ShapeDtypeStruct((width, slices * heads), BF16),
        compiler_params=params(),
        name="slice_attention",
    )(packed, question, lookup, content)


def finish_kernel(
    pos_ref, x_ref, gain, bias, feeder_t, logit_t, sharp_ref, offset_ref, mix_t, emitted, emitted_offset,
    gain2, bias2, entry, entry_offset, leave, leave_offset, *refs, start, per, follows, last,
):
    refs = list(refs)
    before = refs.pop(0) if follows else None
    out_ref, logit_ref, weight_ref, res, dst, sem = refs[:6]
    step = pl.program_id(0)
    sources = x_ref.shape[0]
    block = sources * per
    local = dst.shape[0] // 2

    def handover(inward):
        if inward:
            return pltpu.make_async_copy(before, dst, sem.at[0])
        return pltpu.make_async_copy(dst, out_ref, sem.at[0])

    if follows:

        @pl.when(step == 0)
        def _():
            handover(True).start()

    x = jnp.concatenate([x_ref[s, :per, :] for s in range(sources)], axis=0).astype(F32)
    standard = norm_rows(x, gain[...], bias[...]).astype(BF16)
    slice_weights(standard, feeder_t, logit_t, sharp_ref, offset_ref, logit_ref, weight_ref, None)
    blended_t = jnp.dot(mix_t[...], weight_ref[...], preferred_element_type=F32)
    blended = blended_t.T.astype(BF16)
    hidden = x + jnp.dot(blended, emitted[...], preferred_element_type=F32) + emitted_offset[...]
    normed = norm_rows(hidden, gain2[...], bias2[...]).astype(BF16)
    inner = jnp.dot(normed, entry[...], preferred_element_type=F32) + entry_offset[...]
    active = (inner * (1.0 + lax.erf(inner * math.sqrt(0.5)))).astype(BF16)
    leaving = jnp.dot(active, leave[...], preferred_element_type=F32)
    result = hidden + 0.5 * leaving + leave_offset[...]
    res[:block, :] = result[:, :LANES]
    res[block:, :] = result[:, LANES:]
    if follows:

        @pl.when(step == 0)
        def _():
            handover(True).wait()

    together = max(k for k in range(1, sources + 1) if sources % k == 0 and k * per <= LANES)

    def move(g, carry):
        for q in range(together):
            source = g * together + q
            for j in range(per):
                slot = pos_ref[step * sources + source, start + j]
                row = g * (together * per) + (q * per + j)
                dst[pl.ds(slot, 1), :] = res[pl.ds(row, 1), :]
                dst[pl.ds(slot + local, 1), :] = res[pl.ds(row + block, 1), :]
        return carry

    lax.fori_loop(0, sources // together, move, 0)

    @pl.when(step == pl.num_programs(0) - 1)
    def _():
        if not last:
            handover(False).start()
            handover(False).wait()
        else:
            stage = refs[6]
            parts = sem.shape[0]
            size = local // parts
            copies = []
            for q in range(parts):

                def narrow(c, carry, q=q):
                    row = pl.multiple_of(q * size + c * LANES, LANES)
                    stage[pl.ds(row, LANES), :LANES] = dst[pl.ds(row, LANES), :].astype(BF16)
                    stage[pl.ds(row, LANES), LANES:] = dst[pl.ds(row + local, LANES), :].astype(BF16)
                    return carry

                lax.fori_loop(0, size // LANES, narrow, 0)
                rows = pl.ds(q * size, size)
                copies.append(pltpu.make_async_copy(stage.at[rows], out_ref.at[rows], sem.at[q]))
                copies[-1].start()
            for copy in copies:
                copy.wait()


def finish_rows(positions, arrived, weights, offset, mix_t, rest, before, local, start, per, last):
    devices, stride, width = arrived.shape
    rows = mix_t.shape[1]
    sources = max(k for k in range(1, devices + 1) if devices % k == 0 and k * per <= BLOCK)
    block = sources * per
    follows = before is not None
    shape = (local, width) if last else (2 * local, LANES)
    return pl.pallas_call(
        functools.partial(finish_kernel, start=start, per=per, follows=follows, last=last),
        grid=(devices // sources,),
        in_specs=[
            pl.BlockSpec(memory_space=pltpu.SMEM),
            pl.BlockSpec((sources, stride, width), lambda i: (i, 0, 0)),
            *[whole(w.shape) for w in weights],
            pl.BlockSpec(memory_space=pltpu.SMEM),
            whole(mix_t.shape),
            *[whole(w.shape) for w in rest],
            *([pl.BlockSpec(memory_space=pl.ANY)] if follows else []),
        ],
        out_specs=pl.BlockSpec(memory_space=pl.ANY),
        out_shape=jax.ShapeDtypeStruct(shape, BF16 if last else F32),
        scratch_shapes=[
            pltpu.VMEM((rows, block), F32),
            pltpu.VMEM((rows, block), BF16),
            pltpu.VMEM((2 * block, LANES), F32),
            pltpu.VMEM((2 * local, LANES), F32),
            pltpu.SemaphoreType.DMA((4 if last else 1,)),
            *([pltpu.VMEM((local, width), BF16)] if last else []),
        ],
        compiler_params=params(),
        cost_estimate=pl.CostEstimate(
            flops=2_000_000 * devices * per, bytes_accessed=8_000_000, transcendentals=1000 * devices * per
        ),
    )(positions, arrived, *weights, offset, mix_t, *rest, *([before] if follows else []))


def sum_plane(value, shards):
    step = 1
    while step < shards:
        value = value + lax.ppermute(value, "pts", [(i, i ^ step) for i in range(shards)])
        step *= 2
    return value


def sum_head(value, groups):
    others = [lax.ppermute(value, "head", [(i, i ^ k) for i in range(groups)]) for k in range(1, groups)]
    for other in others:
        value = value + other
    return value


def body(
    layer_inputs_trainorder,
    inference_placement,
    initial_layernorm_gain,
    initial_layernorm_offset,
    attribute_projection,
    assignment_feeder_projection,
    partition_projection,
    partition_offset,
    softmax_sharpness,
    partition_question_map,
    partition_lookup_map,
    partition_content_map,
    emitted_projection,
    emitted_offset,
    latter_layernorm_gain,
    latter_layernorm_offset,
    perceptron_entry_map,
    perceptron_entry_offset,
    perceptron_exit_map,
    perceptron_exit_offset,
):
    groups = lax.axis_size("head")
    shards = lax.axis_size("pts")
    devices = groups * shards
    local, width = layer_inputs_trainorder.shape
    feature, _ = partition_projection.shape
    heads = width // feature
    per = local // devices
    block = 768 if local % 768 == 0 else LANES
    parts = (per // 2, per // 3, per - per // 2 - per // 3)
    starts = (0, parts[0], parts[0] + parts[1])

    def exchange(rows):
        return lax.all_to_all(rows, ("head", "pts"), split_axis=0, concat_axis=0, tiled=True)

    mates = [
        lax.ppermute(softmax_sharpness, "head", [(i, i ^ k) for i in range(groups)])
        for k in range(1, groups)
    ]
    lists, tail = rank_rows(inference_placement, local, width, groups, shards)
    (one,) = gather_rows(lists, layer_inputs_trainorder, tail, starts[0], parts[:1])
    *mates, one = lax.optimization_barrier((*mates, one))
    arrived_one = exchange(one)
    two, three = gather_rows(lists, layer_inputs_trainorder, None, starts[1], parts[1:])

    place = lax.axis_index("head")
    order = jnp.arange(groups)[:, None]
    sharp = jnp.where(order == place, softmax_sharpness[None], 0.0)
    for k, mate in enumerate(mates, 1):
        sharp = jnp.where(order == (place ^ k), mate[None], sharp)
    sharp = (LOG2E / sharp).reshape(heads, 1)
    gain = initial_layernorm_gain[None]
    bias = initial_layernorm_offset[None]
    feeder_t = assignment_feeder_projection.T
    offset = partition_offset[None]
    packed, logit_t = local_sums(
        layer_inputs_trainorder, gain, bias, attribute_projection, feeder_t, partition_projection, sharp,
        offset, block,
    )
    packed = sum_plane(packed, shards)
    _, arrived_one, two = lax.optimization_barrier((packed, arrived_one, two))
    arrived_two = exchange(two)
    packed = sum_head(packed, groups)

    codes = lax.optimization_barrier(arrived_one[:, parts[0] :, :])[:, :2, :per].astype(F32)
    arrived_at = (codes[:, 0] * LANES + codes[:, 1]).astype(jnp.int32)
    mix_t = slice_attention(
        packed, partition_question_map, partition_lookup_map, partition_content_map, heads
    )
    weights = (gain, bias, feeder_t, logit_t, sharp)
    rest = (
        emitted_projection, emitted_offset[None], latter_layernorm_gain[None], latter_layernorm_offset[None],
        perceptron_entry_map, perceptron_entry_offset[None],
        perceptron_exit_map, perceptron_exit_offset[None],
    )
    served = finish_rows(
        arrived_at, arrived_one, weights, offset, mix_t, rest, None, local, starts[0], parts[0], False
    )
    served, arrived_two, three = lax.optimization_barrier((served, arrived_two, three))
    arrived_three = exchange(three)
    served = finish_rows(
        arrived_at, arrived_two, weights, offset, mix_t, rest, served, local, starts[1], parts[1], False
    )
    served = finish_rows(
        arrived_at, arrived_three, weights, offset, mix_t, rest, served, local, starts[2], parts[2], True
    )
    return served[None]


def solution(mesh):
    rows = P(("head", "pts"))
    placed = (P(("head", "pts"), None), rows, *[P()] * 6, P("head"), *[P()] * 11)

    return jax.shard_map(body, mesh=mesh, in_specs=placed, out_specs=P("pts", "head", None), check_vma=False)
```

profile of v0, /device:TPU:0, one launch (start us, length us, event | category | flops | bytes accessed | tf_op | source)
XLA Modules:
  0.0 155.4 jit_solution(7256120274148980374)
XLA Ops:
  0.0 4.1 %collective-permute-start.1 = (f32[4]{0:T(128)}, f32[4]{0:T(128)S(1)}, u32[]{:S(2)}, u32[]{:S(2)}) collective-permute-start(f32[4]{0:T(128)} %param.28), channel_id=1, source_target_pairs={{0,16},{8,24},{16,0},{24,8},{1,17},{9,25},{17,1},{25,9},{2,18},{10... | collective-permute-start | bytes 56 | tf_op jit(solution)/shard_map/ppermute | solution.py:499
  4.1 1.6 %collective-permute-start = (f32[4]{0:T(128)}, f32[4]{0:T(128)S(1)}, u32[]{:S(2)}, u32[]{:S(2)}) collective-permute-start(f32[4]{0:T(128)} %param.28), channel_id=1, source_target_pairs={{0,8},{8,0},{16,24},{24,16},{1,9},{9,1},{17,25},{25,17},{2,10},{10... | collective-permute-start | bytes 56 | tf_op jit(solution)/shard_map/ppermute | solution.py:499
  5.6 5.8 %rank_rows.1 = (s32[32,256]{1,0:T(8,128)}, f32[64,256]{1,0:T(8,128)}) custom-call(s32[48,128]{1,0:T(8,128)} %bitcast.17), custom_call_target="tpu_custom_call" | custom-call | tf_op jit(solution)/shard_map/rank_rows/pallas_call | solution.py:96
  11.5 7.4 %gather_first.1 = bf16[32,104,256]{2,1,0:T(8,128)(2,1)} custom-call(s32[32,256]{1,0:T(8,128)} %get-tuple-element.20.list_ref, bf16[6144,256]{1,0:T(8,128)(2,1)} %x_ref.5, f32[64,256]{1,0:T(8,128)} %get-tuple-element.21.refs_0_), custom_call_target="tpu_custom_call" | custom-call | flops 6144000000 | bytes 6000000 | tf_op jit(solution)/shard_map/gather_first/pallas_call | solution.py:157
  19.0 6.1 %all-to-all-start = ((bf16[32,104,256]{2,1,0:T(8,128)(2,1)}), bf16[32,104,256]{2,1,0:T(8,128)(2,1)S(1)}, u32[]{:S(2)}, u32[]{:S(2)}) async-start(bf16[32,104,256]{2,1,0:T(8,128)(2,1)} %gather_first.1), calls=%async_computation | async-start | bytes 3407872 | tf_op jit(solution)/shard_map/all_to_all | solution.py:496
  26.6 16.0 %local_sums.1 = (f32[32,384]{1,0:T(8,128)}, bf16[512,256]{1,0:T(8,128)(2,1)}) custom-call(bf16[6144,256]{1,0:T(8,128)(2,1)} %x_ref.5, f32[1,256]{1,0:T(1,128)} %bitcast.21, f32[1,256]{1,0:T(1,128)} %bitcast.25, bf16[256,256]{1,0:T(8,128)(2,1)} %attribute.1, bf16[256,256]{1,0:T(8,128)(2,1)} %bitcast.13, bf16[16,32]{1,0:T(8,128)(2,1)} %partition.1, ...), custom_call_target="tpu_custom_call" | custom-call | flops 5000000000 | bytes 4000000 | tf_op jit(solution)/shard_map/local_sums/pallas_call | solution.py:256
  42.9 1.2 collective-permute-done.3
  44.1 0.8 add.22
  44.9 1.8 %collective-permute-start.4 = (f32[32,384]{1,0:T(8,128)S(1)}, f32[32,384]{1,0:T(8,128)S(1)}, u32[]{:S(2)}, u32[]{:S(2)}) collective-permute-start(f32[32,384]{1,0:T(8,128)S(1)} %add.22), channel_id=1, source_target_pairs={{0,2},{1,3},{2,0},{3,1},{4,6},{5,7},{6,4},{7,5},{8,10},{9,11},{10,... | collective-permute-start | bytes 147464 | tf_op jit(solution)/shard_map/ppermute | solution.py:450
  46.6 2.5 %collective-permute-done.4 = f32[32,384]{1,0:T(8,128)S(1)} collective-permute-done((f32[32,384]{1,0:T(8,128)S(1)}, f32[32,384]{1,0:T(8,128)S(1)}, u32[]{:S(2)}, u32[]{:S(2)}) %collective-permute-start.4) | collective-permute-done | bytes 49184 | tf_op jit(solution)/shard_map/ppermute | solution.py:450
  49.1 1.7 %collective-permute-start.5 = (f32[32,384]{1,0:T(8,128)S(1)}, f32[32,384]{1,0:T(8,128)S(1)}, u32[]{:S(2)}, u32[]{:S(2)}) collective-permute-start(f32[32,384]{1,0:T(8,128)S(1)} %add.23), channel_id=1, source_target_pairs={{0,4},{1,5},{2,6},{3,7},{4,0},{5,1},{6,2},{7,3},{8,12},{9,13},{10,... | collective-permute-start | bytes 147464 | tf_op jit(solution)/shard_map/ppermute | solution.py:450
  50.8 7.4 %gather_rest.1 = (bf16[32,64,256]{2,1,0:T(8,128)(2,1)}, bf16[32,32,256]{2,1,0:T(8,128)(2,1)}) custom-call(s32[32,256]{1,0:T(8,128)} %get-tuple-element.20.list_ref, bf16[6144,256]{1,0:T(8,128)(2,1)} %x_ref.5), custom_call_target="tpu_custom_call" | custom-call | flops 6144000000 | bytes 6000000 | tf_op jit(solution)/shard_map/gather_rest/pallas_call | solution.py:157
  58.3 7.2 %all-to-all-done.x_ref = bf16[32,104,256]{2,1,0:T(8,128)(2,1)S(1)} async-done(((bf16[32,104,256]{2,1,0:T(8,128)(2,1)}), bf16[32,104,256]{2,1,0:T(8,128)(2,1)S(1)}, u32[]{:S(2)}, u32[]{:S(2)}) %all-to-all-start) | async-done | bytes 1703968 | tf_op jit(solution)/shard_map/all_to_all | solution.py:496
  65.5 4.1 %all-to-all-start.1 = ((bf16[32,64,256]{2,1,0:T(8,128)(2,1)}), bf16[32,64,256]{2,1,0:T(8,128)(2,1)S(1)}, u32[]{:S(2)}, u32[]{:S(2)}) async-start(bf16[32,64,256]{2,1,0:T(8,128)(2,1)} %get-tuple-element.30), calls=%async_computation.1 | async-start | bytes 2097152 | tf_op jit(solution)/shard_map/all_to_all | solution.py:496
  69.6 3.5 %collective-permute-start.8 = (f32[32,384]{1,0:T(8,128)S(1)}, f32[32,384]{1,0:T(8,128)S(1)}, u32[]{:S(2)}, u32[]{:S(2)}) collective-permute-start(f32[32,384]{1,0:T(8,128)S(1)} %add.24), channel_id=1, source_target_pairs={{0,24},{8,16},{16,8},{24,0},{1,25},{9,17},{17,9},{25,1},{2,26},{10... | collective-permute-start | bytes 147464 | tf_op jit(solution)/shard_map/ppermute | solution.py:456
  73.1 0.9 collective-permute-start.6
  74.0 18.5 %collective-permute-done.8 = f32[32,384]{1,0:T(8,128)S(1)} collective-permute-done((f32[32,384]{1,0:T(8,128)S(1)}, f32[32,384]{1,0:T(8,128)S(1)}, u32[]{:S(2)}, u32[]{:S(2)}) %collective-permute-start.8) | collective-permute-done | bytes 49184 | tf_op jit(solution)/shard_map/ppermute | solution.py:456
  92.5 7.3 %collective-permute-done.7 = f32[32,384]{1,0:T(8,128)S(1)} collective-permute-done((f32[32,384]{1,0:T(8,128)S(1)}, f32[32,384]{1,0:T(8,128)S(1)}, u32[]{:S(2)}, u32[]{:S(2)}) %collective-permute-start.7) | collective-permute-done | bytes 49184 | tf_op jit(solution)/shard_map/ppermute | solution.py:456
  100.4 4.2 %slice_attention.1.mix_t = bf16[256,512]{1,0:T(8,128)(2,1)} custom-call(f32[32,384]{1,0:T(8,128)} %add_add_fusion.packed_ref, f32[16,16]{1,0:T(8,128)} %question.1, f32[16,16]{1,0:T(8,128)} %lookup.1, f32[16,16]{1,0:T(8,128)} %content.1), custom_call_target="tpu_custom_call" | custom-call | tf_op jit(solution)/shard_map/slice_attention/pallas_call | solution.py:321
  105.7 20.6 %shard_map.190.refs_0_ = f32[12288,128]{1,0:T(8,128)} custom-call(s32[32,192]{1,0:T(8,128)} %fusion.1.pos_ref, bf16[32,104,256]{2,1,0:T(8,128)(2,1)} %copy-done, f32[1,256]{1,0:T(1,128)} %bitcast.22, f32[1,256]{1,0:T(1,128)} %bitcast.26, bf16[256,256]{1,0:T(8,128)(2,1)} %bitcast.14, bf16[512,256]{1,0:T(8,128)(2,1)} %get-tuple-element.29.logit_t, ...), custom_call_target="tpu_custom_call" | custom-call | flops 6144000000 | bytes 8000000 | tf_op jit(solution)/shard_map/pallas_call | solution.py:418
  126.4 3.8 %all-to-all-start.2 = ((bf16[32,32,256]{2,1,0:T(8,128)(2,1)}), bf16[32,32,256]{2,1,0:T(8,128)(2,1)S(1)}, u32[]{:S(2)}, u32[]{:S(2)}) async-start(bf16[32,32,256]{2,1,0:T(8,128)(2,1)} %get-tuple-element.32), calls=%async_computation.2 | async-start | bytes 1048576 | tf_op jit(solution)/shard_map/all_to_all | solution.py:496
  130.2 14.8 %shard_map.191.refs_0_ = f32[12288,128]{1,0:T(8,128)} custom-call(s32[32,192]{1,0:T(8,128)} %fusion.1.pos_ref, bf16[32,64,256]{2,1,0:T(8,128)(2,1)} %copy-done.1, f32[1,256]{1,0:T(1,128)} %bitcast.23, f32[1,256]{1,0:T(1,128)} %bitcast.27, bf16[256,256]{1,0:T(8,128)(2,1)} %bitcast.15, bf16[512,256]{1,0:T(8,128)(2,1)} %get-tuple-element.29.logit_t, ...), custom_call_target="tpu_custom_call" | custom-call | flops 4096000000 | bytes 8000000 | tf_op jit(solution)/shard_map/pallas_call | solution.py:418
  145.6 0.8 copy-done.2
  146.4 8.8 %shard_map.192 = bf16[6144,256]{1,0:T(8,128)(2,1)} custom-call(s32[32,192]{1,0:T(8,128)} %fusion.1.pos_ref, bf16[32,32,256]{2,1,0:T(8,128)(2,1)} %copy-done.2, f32[1,256]{1,0:T(1,128)} %bitcast.24, f32[1,256]{1,0:T(1,128)} %bitcast.28, bf16[256,256]{1,0:T(8,128)(2,1)} %bitcast.16, bf16[512,256]{1,0:T(8,128)(2,1)} %get-tuple-element.29.logit_t, ...), custom_call_target="tpu_custom_call" | custom-call | flops 2048000000 | bytes 8000000 | tf_op jit(solution)/shard_map/pallas_call | solution.py:418
  (31 shorter events, 4.1 us)
Async XLA Ops:
  0.0 18.9 %collective-permute-start.1 = (f32[4]{0:T(128)}, f32[4]{0:T(128)S(1)}, u32[]{:S(2)}, u32[]{:S(2)}) collective-permute-start(f32[4]{0:T(128)} %param.28), channel_id=1, source_target_pairs={{0,16},{8,24},{16,0},{24,8},{1,17},{9,25},{17,1},{25,9},{2,18},{10... | collective-permute-start | bytes 56 | tf_op jit(solution)/shard_map/ppermute | solution.py:499
  4.1 14.9 %collective-permute-start = (f32[4]{0:T(128)}, f32[4]{0:T(128)S(1)}, u32[]{:S(2)}, u32[]{:S(2)}) collective-permute-start(f32[4]{0:T(128)} %param.28), channel_id=1, source_target_pairs={{0,8},{8,0},{16,24},{24,16},{1,9},{9,1},{17,25},{25,17},{2,10},{10... | collective-permute-start | bytes 56 | tf_op jit(solution)/shard_map/ppermute | solution.py:499
  5.6 13.3 %collective-permute-start.2 = (f32[4]{0:T(128)}, f32[4]{0:T(128)S(1)}, u32[]{:S(2)}, u32[]{:S(2)}) collective-permute-start(f32[4]{0:T(128)} %param.28), channel_id=1, source_target_pairs={{0,24},{8,16},{16,8},{24,0},{1,25},{9,17},{17,9},{25,1},{2,26},{10... | collective-permute-start | bytes 56 | tf_op jit(solution)/shard_map/ppermute | solution.py:499
  18.9 6.1 %copy-start.3 = (bf16[256,256]{1,0:T(8,128)(2,1)S(1)}, bf16[256,256]{1,0:T(8,128)(2,1)}, u32[]{:S(2)}) copy-start(bf16[256,256]{1,0:T(8,128)(2,1)} %param.25) | copy-start | bytes 393220
  18.9 6.9 %copy-start.4 = (f32[4]{0:T(128)S(1)}, f32[4]{0:T(128)}, u32[]{:S(2)}) copy-start(f32[4]{0:T(128)} %param.28) | copy-start | bytes 52
  19.0 46.5 %all-to-all-start = ((bf16[32,104,256]{2,1,0:T(8,128)(2,1)}), bf16[32,104,256]{2,1,0:T(8,128)(2,1)S(1)}, u32[]{:S(2)}, u32[]{:S(2)}) async-start(bf16[32,104,256]{2,1,0:T(8,128)(2,1)} %gather_first.1), calls=%async_computation | async-start | bytes 3407872 | tf_op jit(solution)/shard_map/all_to_all | solution.py:496
  42.6 1.4 collective-permute-start.3
  44.9 4.3 %collective-permute-start.4 = (f32[32,384]{1,0:T(8,128)S(1)}, f32[32,384]{1,0:T(8,128)S(1)}, u32[]{:S(2)}, u32[]{:S(2)}) collective-permute-start(f32[32,384]{1,0:T(8,128)S(1)} %add.22), channel_id=1, source_target_pairs={{0,2},{1,3},{2,0},{3,1},{4,6},{5,7},{6,4},{7,5},{8,10},{9,11},{10,... | collective-permute-start | bytes 147464 | tf_op jit(solution)/shard_map/ppermute | solution.py:450
  49.1 9.1 %collective-permute-start.5 = (f32[32,384]{1,0:T(8,128)S(1)}, f32[32,384]{1,0:T(8,128)S(1)}, u32[]{:S(2)}, u32[]{:S(2)}) collective-permute-start(f32[32,384]{1,0:T(8,128)S(1)} %add.23), channel_id=1, source_target_pairs={{0,4},{1,5},{2,6},{3,7},{4,0},{5,1},{6,2},{7,3},{8,12},{9,13},{10,... | collective-permute-start | bytes 147464 | tf_op jit(solution)/shard_map/ppermute | solution.py:450
  65.5 39.6 %copy-start = (bf16[32,104,256]{2,1,0:T(8,128)(2,1)}, bf16[32,104,256]{2,1,0:T(8,128)(2,1)S(1)}, u32[]{:S(2)}) copy-start(bf16[32,104,256]{2,1,0:T(8,128)(2,1)S(1)} %all-to-all-done.x_ref) | copy-start | bytes 5111812
  65.5 60.9 %all-to-all-start.1 = ((bf16[32,64,256]{2,1,0:T(8,128)(2,1)}), bf16[32,64,256]{2,1,0:T(8,128)(2,1)S(1)}, u32[]{:S(2)}, u32[]{:S(2)}) async-start(bf16[32,64,256]{2,1,0:T(8,128)(2,1)} %get-tuple-element.30), calls=%async_computation.1 | async-start | bytes 2097152 | tf_op jit(solution)/shard_map/all_to_all | solution.py:496
  69.6 23.0 %collective-permute-start.8 = (f32[32,384]{1,0:T(8,128)S(1)}, f32[32,384]{1,0:T(8,128)S(1)}, u32[]{:S(2)}, u32[]{:S(2)}) collective-permute-start(f32[32,384]{1,0:T(8,128)S(1)} %add.24), channel_id=1, source_target_pairs={{0,24},{8,16},{16,8},{24,0},{1,25},{9,17},{17,9},{25,1},{2,26},{10... | collective-permute-start | bytes 147464 | tf_op jit(solution)/shard_map/ppermute | solution.py:456
  73.1 26.7 %collective-permute-start.7 = (f32[32,384]{1,0:T(8,128)S(1)}, f32[32,384]{1,0:T(8,128)S(1)}, u32[]{:S(2)}, u32[]{:S(2)}) collective-permute-start(f32[32,384]{1,0:T(8,128)S(1)} %add.24), channel_id=1, source_target_pairs={{0,16},{8,24},{16,0},{24,8},{1,17},{9,25},{17,1},{25,9},{2,18},{10... | collective-permute-start | bytes 147464 | tf_op jit(solution)/shard_map/ppermute | solution.py:456
  73.1 26.7 %collective-permute-start.6 = (f32[32,384]{1,0:T(8,128)S(1)}, f32[32,384]{1,0:T(8,128)S(1)}, u32[]{:S(2)}, u32[]{:S(2)}) collective-permute-start(f32[32,384]{1,0:T(8,128)S(1)} %add.24), channel_id=1, source_target_pairs={{0,8},{8,0},{16,24},{24,16},{1,9},{9,1},{17,25},{25,17},{2,10},{10... | collective-permute-start | bytes 147464 | tf_op jit(solution)/shard_map/ppermute | solution.py:456
  126.3 3.9 %copy-start.1 = (bf16[32,64,256]{2,1,0:T(8,128)(2,1)}, bf16[32,64,256]{2,1,0:T(8,128)(2,1)S(1)}, u32[]{:S(2)}) copy-start(bf16[32,64,256]{2,1,0:T(8,128)(2,1)S(1)} %all-to-all-done.1.x_ref) | copy-start | bytes 3145732
  126.4 19.2 %all-to-all-start.2 = ((bf16[32,32,256]{2,1,0:T(8,128)(2,1)}), bf16[32,32,256]{2,1,0:T(8,128)(2,1)S(1)}, u32[]{:S(2)}, u32[]{:S(2)}) async-start(bf16[32,32,256]{2,1,0:T(8,128)(2,1)} %get-tuple-element.32), calls=%async_computation.2 | async-start | bytes 1048576 | tf_op jit(solution)/shard_map/all_to_all | solution.py:496
  145.6 0.8 copy-start.2
where the time goes:
time: 156 us; the launch traced here: 155 us
  Pallas kernels  85.1 us (55%)
  waiting for transfers between devices  37.3 us (24%)
  starting transfers between devices  27.8 us (18%)
  local copies, waits for them, and re-layouts  2.66 us (2%)
  other arithmetic  2.17 us (1%)
    pallas_call x3, Pallas kernels, finish_rows(): pl.pallas_call(functools.partial(finish_kernel, start=start, per=per, fol...  44.2 us
    ppermute x3, waiting for transfers between devices, sum_head(): lax.ppermute(value, 'head', [(i, i ^ k) for i in range(groups)])  25.8 us
    pallas_call x1, Pallas kernels, local_sums(): pl.pallas_call(sums_kernel, grid=(local // block,), in_specs=[pl.BlockSpe...  16 us
    pallas_call x2, Pallas kernels, gather_rows(): pl.pallas_call(functools.partial(gather_kernel, start=start, counts=count...  14.9 us
    all_to_all x3, starting transfers between devices, exchange(): lax.all_to_all(rows, ('head', 'pts'), split_axis=0, concat_axis=0, tiled=...  14 us
    all_to_all x3, waiting for transfers between devices, exchange(): lax.all_to_all(rows, ('head', 'pts'), split_axis=0, concat_axis=0, tiled=...  7.82 us
    pallas_call x1, Pallas kernels, rank_rows(): pl.pallas_call(functools.partial(rank_kernel, local=local, groups=groups,...  5.83 us
    ppermute x3, starting transfers between devices, body(): lax.ppermute(softmax_sharpness, 'head', [(i, i ^ k) for i in range(groups)])  5.64 us
  transfers between devices with their start and end apart: 12, of which 6 were waited for; matrix products, arithmetic and copies ran while one was open for 3% of the time, Pallas kernels for 49%

commit v1 on v0

--- a/solution.py
+++ b/solution.py
@@ -41,10 +41,52 @@
     return centred * lax.rsqrt(spread + EPS_NORM) * gain + bias
 
 
-def rank_kernel(place_ref, list_ref, tail_ref, hot_ref, count_ref, key_ref, *, local, groups, shards):
+def narrow_rows(source, first, other, count):
+    low = source[first : first + count, :].astype(BF16)
+    return low, source[other : other + count, :].astype(BF16)
+
+
+def fetch_rows(lists, start, count, src, dst, stage, out, sem, group):
+    local = src.shape[0] // 2
+    devices = lists.shape[0]
+    copies = []
+    for d in range(devices):
+        base = (d % 2) * 2 * count
+        for j in range(count):
+            row = lists[d, start + j]
+            dst[base + j : base + j + 1, :] = src[pl.ds(row, 1), :]
+            dst[base + count + j : base + count + j + 1, :] = src[pl.ds(row + local, 1), :]
+        stage[d, :count, :LANES], stage[d, :count, LANES:] = narrow_rows(dst, base, base + count, count)
+        if (d + 1) % group == 0:
+            part = pl.ds(d + 1 - group, group)
+            copies.append(pltpu.make_async_copy(stage.at[part], out.at[part], sem.at[d // group]))
+            copies[-1].start()
+    for copy in copies:
+        copy.wait()
+
+
+def widen_rows(x_ref, src):
+    local = x_ref.shape[0]
+
+    def widen(c, carry):
+        row = pl.multiple_of(c * LANES, LANES)
+        src[pl.ds(row, LANES), :] = x_ref[pl.ds(row, LANES), :LANES].astype(F32)
+        src[pl.ds(row + local, LANES), :] = x_ref[pl.ds(row, LANES), LANES:].astype(F32)
+        return carry
+
+    lax.fori_loop(0, local // LANES, widen, 0)
+
+
+def send_kernel(
+    place_ref, x_hbm, list_ref, out, hot_ref, count_ref, key_ref, x_ref, src, dst, stage, list_s, sem,
+    *, groups, shards, first,
+):
     devices = groups * shards
     chunks = place_ref.shape[0]
     padded = list_ref.shape[1]
+    local, width = x_ref.shape
+    rows_in = pltpu.make_async_copy(x_hbm, x_ref, sem.at[0])
+    rows_in.start()
     placement = place_ref[...].astype(F32)
     block = floor_div(placement, local)
     within = placement - block * local
@@ -81,93 +123,82 @@
                 chosen, value, 0.0
             ).astype(BF16)
     codes = lax.dot_general(hot_ref[...], key_ref[...], NT, preferred_element_type=F32)
-    tail_ref[...] = jnp.zeros_like(tail_ref)
-    tail_ref[:devices, :padded] = codes[:, :padded]
-    tail_ref[devices:, :padded] = codes[:, padded : 2 * padded]
     source = codes[:, 2 * padded : 3 * padded] * LANES + codes[:, 3 * padded :]
     list_ref[...] = source.astype(jnp.int32)
-
-
-def rank_rows(placement, local, width, groups, shards):
+    lists_in = pltpu.make_async_copy(list_ref, list_s, sem.at[1])
+    lists_in.start()
+    line = lax.broadcasted_iota(jnp.int32, (TAIL, padded), 0)
+    for d in range(devices):
+        tail = jnp.where(
+            line == 0, codes[d : d + 1, :padded], jnp.where(line == 1, codes[d : d + 1, padded : 2 * padded], 0.0)
+        )
+        if padded < width:
+            tail = jnp.concatenate([tail, jnp.zeros((TAIL, width - padded), F32)], axis=1)
+        stage[d, first:, :] = tail.astype(BF16)
+    rows_in.wait()
+    widen_rows(x_ref, src)
+    lists_in.wait()
+    fetch_rows(list_s, 0, first, src, dst, stage, out, sem, devices // sem.shape[0])
+
+
+def send_first(placement, rows, groups, shards, first):
     devices = groups * shards
-    per = local // devices
-    padded = -(-per // LANES) * LANES
+    local, width = rows.shape
+    padded = -(-(local // devices) // LANES) * LANES
     chunks = local // LANES
+    vmem = pl.BlockSpec(memory_space=pltpu.VMEM)
+    hbm = pl.BlockSpec(memory_space=pl.ANY)
     return pl.pallas_call(
-        functools.partial(rank_kernel, local=local, groups=groups, shards=shards),
+        functools.partial(send_kernel, groups=groups, shards=shards, first=first),
+        in_specs=[vmem, hbm],
+        out_specs=(vmem, hbm),
         out_shape=(
             jax.ShapeDtypeStruct((devices, padded), jnp.int32),
-            jax.ShapeDtypeStruct((2 * devices, width), F32),
+            jax.ShapeDtypeStruct((devices, first + TAIL, width), BF16),
         ),
         scratch_shapes=[
             pltpu.VMEM((devices, local), BF16),
             pltpu.VMEM((chunks * devices, 2 * LANES), F32),
             pltpu.VMEM((4 * padded, local), BF16),
+            pltpu.VMEM((local, width), BF16),
+            pltpu.VMEM((2 * local, LANES), F32),
+            pltpu.VMEM((4 * first, LANES), F32),
+            pltpu.VMEM((devices, first + TAIL, width), BF16),
+            pltpu.SMEM((devices, padded), jnp.int32),
+            pltpu.SemaphoreType.DMA((4,)),
         ],
         compiler_params=params(),
-        name="rank_rows",
-    )(placement.reshape(chunks, LANES))
-
-
-def gather_kernel(list_ref, x_ref, *refs, start, counts, tailed):
-    tail_ref = refs[0] if tailed else None
-    outs = refs[1 if tailed else 0 : -2]
-    src, dst = refs[-2:]
-    local, width = x_ref.shape
-    devices = list_ref.shape[0]
-    total = sum(counts)
-
-    def widen(c, carry):
-        row = pl.multiple_of(c * LANES, LANES)
-        src[pl.ds(row, LANES), :] = x_ref[pl.ds(row, LANES), :LANES].astype(F32)
-        src[pl.ds(row + local, LANES), :] = x_ref[pl.ds(row, LANES), LANES:].astype(F32)
-        return carry
-
-    lax.fori_loop(0, local // LANES, widen, 0)
-    line = lax.broadcasted_iota(jnp.int32, (TAIL, width), 0)
-
-    def fetch(d, carry):
-        for j in range(total):
-            row = list_ref[d, start + j]
-            dst[j : j + 1, :] = src[pl.ds(row, 1), :]
-            dst[total + j : total + j + 1, :] = src[pl.ds(row + local, 1), :]
-        done = 0
-        for out, count in zip(outs, counts):
-            out[d, :count, :LANES] = dst[done : done + count, :].astype(BF16)
-            out[d, :count, LANES:] = dst[total + done : total + done + count, :].astype(BF16)
-            done += count
-        if tailed:
-            high = tail_ref[pl.ds(d, 1), :]
-            low = tail_ref[pl.ds(d + devices, 1), :]
-            codes = jnp.where(line == 0, high, jnp.where(line == 1, low, 0.0))
-            outs[0][d, counts[0] :, :] = codes.astype(BF16)
-        return carry
-
-    lax.fori_loop(0, devices, fetch, 0)
-
-
-def gather_rows(lists, rows, tail, start, counts):
+        name="send_first",
+    )(placement.reshape(chunks, LANES), rows)
+
+
+def rest_kernel(list_ref, x_ref, out, src, dst, stage, sem, *, first):
+    widen_rows(x_ref, src)
+    fetch_rows(
+        list_ref, first, out.shape[1], src, dst, stage, out, sem, list_ref.shape[0] // sem.shape[0]
+    )
+
+
+def send_rest(lists, rows, first, count):
     local, width = rows.shape
     devices = lists.shape[0]
-    tailed = tail is not None
-    vmem = pl.BlockSpec(memory_space=pltpu.VMEM)
-    out_shape = [
-        jax.ShapeDtypeStruct((devices, n + (TAIL if tailed else 0), width), BF16) for n in counts
-    ]
     return pl.pallas_call(
-        functools.partial(gather_kernel, start=start, counts=counts, tailed=tailed),
-        in_specs=[pl.BlockSpec(memory_space=pltpu.SMEM), vmem, *([vmem] if tailed else [])],
-        out_shape=out_shape,
+        functools.partial(rest_kernel, first=first),
+        in_specs=[pl.BlockSpec(memory_space=pltpu.SMEM), pl.BlockSpec(memory_space=pltpu.VMEM)],
+        out_specs=pl.BlockSpec(memory_space=pl.ANY),
+        out_shape=jax.ShapeDtypeStruct((devices, count, width), BF16),
         scratch_shapes=[
             pltpu.VMEM((2 * local, LANES), F32),
-            pltpu.VMEM((2 * sum(counts), LANES), F32),
+            pltpu.VMEM((4 * count, LANES), F32),
+            pltpu.VMEM((devices, count, width), BF16),
+            pltpu.SemaphoreType.DMA((4,)),
         ],
         compiler_params=params(),
         cost_estimate=pl.CostEstimate(
-            flops=2_000_000 * devices * sum(counts), bytes_accessed=6_000_000, transcendentals=0
+            flops=2_000_000 * devices * count, bytes_accessed=6_000_000, transcendentals=0
         ),
-        name="gather_first" if tailed else "gather_rest",
-    )(lists, rows, *([tail] if tailed else []))
+        name="send_rest",
+    )(lists, rows)
 
 
 def slice_weights(standard, feeder_t, logit_t, sharp_ref, offset_ref, logit_ref, weight_ref, total_ref):
@@ -327,16 +358,21 @@
 
 
 def finish_kernel(
-    pos_ref, x_ref, gain, bias, feeder_t, logit_t, sharp_ref, offset_ref, mix_t, emitted, emitted_offset,
+    pos_hbm, x_ref, gain, bias, feeder_t, logit_t, sharp_ref, offset_ref, mix_t, emitted, emitted_offset,
     gain2, bias2, entry, entry_offset, leave, leave_offset, *refs, start, per, follows, last,
 ):
     refs = list(refs)
     before = refs.pop(0) if follows else None
-    out_ref, logit_ref, weight_ref, res, dst, sem = refs[:6]
+    out_ref, logit_ref, weight_ref, res, dst, pos_ref, sem, pos_sem = refs[:8]
     step = pl.program_id(0)
     sources = x_ref.shape[0]
     block = sources * per
     local = dst.shape[0] // 2
+
+    slots_in = pltpu.make_async_copy(
+        pos_hbm.at[pl.ds(pl.multiple_of(step * sources, 8), sources)], pos_ref, pos_sem.at[0]
+    )
+    slots_in.start()
 
     def handover(inward):
         if inward:
@@ -368,19 +404,13 @@
         def _():
             handover(True).wait()
 
-    together = max(k for k in range(1, sources + 1) if sources % k == 0 and k * per <= LANES)
-
-    def move(g, carry):
-        for q in range(together):
-            source = g * together + q
-            for j in range(per):
-                slot = pos_ref[step * sources + source, start + j]
-                row = g * (together * per) + (q * per + j)
-                dst[pl.ds(slot, 1), :] = res[pl.ds(row, 1), :]
-                dst[pl.ds(slot + local, 1), :] = res[pl.ds(row + block, 1), :]
-        return carry
-
-    lax.fori_loop(0, sources // together, move, 0)
+    slots_in.wait()
+    for source in range(sources):
+        for j in range(per):
+            slot = pos_ref[source, start + j]
+            row = source * per + j
+            dst[pl.ds(slot, 1), :] = res[row : row + 1, :]
+            dst[pl.ds(slot + local, 1), :] = res[row + block : row + block + 1, :]
 
     @pl.when(step == pl.num_programs(0) - 1)
     def _():
@@ -388,7 +418,7 @@
             handover(False).start()
             handover(False).wait()
         else:
-            stage = refs[6]
+            stage = refs[8]
             parts = sem.shape[0]
             size = local // parts
             copies = []
@@ -411,7 +441,10 @@
 def finish_rows(positions, arrived, weights, offset, mix_t, rest, before, local, start, per, last):
     devices, stride, width = arrived.shape
     rows = mix_t.shape[1]
-    sources = max(k for k in range(1, devices + 1) if devices % k == 0 and k * per <= BLOCK)
+    sources = max(
+        k for k in range(8, devices + 1, 8)
+        if devices % k == 0 and k * per <= BLOCK and k * per % LANES == 0
+    )
     block = sources * per
     follows = before is not None
     shape = (local, width) if last else (2 * local, LANES)
@@ -419,7 +452,7 @@
         functools.partial(finish_kernel, start=start, per=per, follows=follows, last=last),
         grid=(devices // sources,),
         in_specs=[
-            pl.BlockSpec(memory_space=pltpu.SMEM),
+            pl.BlockSpec(memory_space=pl.ANY),
             pl.BlockSpec((sources, stride, width), lambda i: (i, 0, 0)),
             *[whole(w.shape) for w in weights],
             pl.BlockSpec(memory_space=pltpu.SMEM),
@@ -434,7 +467,9 @@
             pltpu.VMEM((rows, block), BF16),
             pltpu.VMEM((2 * block, LANES), F32),
             pltpu.VMEM((2 * local, LANES), F32),
+            pltpu.SMEM((sources, positions.shape[1]), jnp.int32),
             pltpu.SemaphoreType.DMA((4 if last else 1,)),
+            pltpu.SemaphoreType.DMA((1,)),
             *([pltpu.VMEM((local, width), BF16)] if last else []),
         ],
         compiler_params=params(),
@@ -489,8 +524,8 @@
     heads = width // feature
     per = local // devices
     block = 768 if local % 768 == 0 else LANES
-    parts = (per // 2, per // 3, per - per // 2 - per // 3)
-    starts = (0, parts[0], parts[0] + parts[1])
+    first = per * 7 // 12 // 8 * 8
+    second = per - first
 
     def exchange(rows):
         return lax.all_to_all(rows, ("head", "pts"), split_axis=0, concat_axis=0, tiled=True)
@@ -499,11 +534,10 @@
         lax.ppermute(softmax_sharpness, "head", [(i, i ^ k) for i in range(groups)])
         for k in range(1, groups)
     ]
-    lists, tail = rank_rows(inference_placement, local, width, groups, shards)
-    (one,) = gather_rows(lists, layer_inputs_trainorder, tail, starts[0], parts[:1])
+    lists, one = send_first(inference_placement, layer_inputs_trainorder, groups, shards, first)
     *mates, one = lax.optimization_barrier((*mates, one))
     arrived_one = exchange(one)
-    two, three = gather_rows(lists, layer_inputs_trainorder, None, starts[1], parts[1:])
+    two = send_rest(lists, layer_inputs_trainorder, first, second)
 
     place = lax.axis_index("head")
     order = jnp.arange(groups)[:, None]
@@ -524,7 +558,7 @@
     arrived_two = exchange(two)
     packed = sum_head(packed, groups)
 
-    codes = lax.optimization_barrier(arrived_one[:, parts[0] :, :])[:, :2, :per].astype(F32)
+    codes = lax.optimization_barrier(arrived_one[:, first:, :])[:, :2, :].astype(F32)
     arrived_at = (codes[:, 0] * LANES + codes[:, 1]).astype(jnp.int32)
     mix_t = slice_attention(
         packed, partition_question_map, partition_lookup_map, partition_content_map, heads
@@ -536,15 +570,10 @@
         perceptron_exit_map, perceptron_exit_offset[None],
     )
     served = finish_rows(
-        arrived_at, arrived_one, weights, offset, mix_t, rest, None, local, starts[0], parts[0], False
-    )
-    served, arrived_two, three = lax.optimization_barrier((served, arrived_two, three))
-    arrived_three = exchange(three)
+        arrived_at, arrived_one, weights, offset, mix_t, rest, None, local, 0, first, False
+    )
     served = finish_rows(
-        arrived_at, arrived_two, weights, offset, mix_t, rest, served, local, starts[1], parts[1], False
-    )
-    served = finish_rows(
-        arrived_at, arrived_three, weights, offset, mix_t, rest, served, local, starts[2], parts[2], True
+        arrived_at, arrived_two, weights, offset, mix_t, rest, served, local, first, second, True
     )
     return served[None]
 

time: 156 us -> 156 us (level)
  waiting for transfers between devices: 37.3 us -> 50.7 us
  Pallas kernels: 85.1 us -> 77 us
  starting transfers between devices: 27.8 us -> 22.2 us
    pallas_call x3 -> x2, Pallas kernels: 44.2 us -> 37.8 us  [finish_rows(): pl.pallas_call(functools.partial(finish_kernel, start=start, per=per, fol...]
    ppermute x3, waiting for transfers between devices: 25.8 us -> 31.4 us  [sum_head(): lax.ppermute(value, 'head', [(i, i ^ k) for i in range(groups)])]
    all_to_all x3 -> x2, waiting for transfers between devices: 7.82 us -> 12.8 us  [exchange(): lax.all_to_all(rows, ('head', 'pts'), split_axis=0, concat_axis=0, tiled=...]
    all_to_all x3 -> x2, starting transfers between devices: 14 us -> 10.3 us  [exchange(): lax.all_to_all(rows, ('head', 'pts'), split_axis=0, concat_axis=0, tiled=...]
    ppermute x3, waiting for transfers between devices: 3.69 us -> 6.38 us  [sum_plane(): lax.ppermute(value, 'pts', [(i, i ^ step) for i in range(shards)])]
    ppermute x3, starting transfers between devices: 3.68 us -> 1.75 us  [sum_plane(): lax.ppermute(value, 'pts', [(i, i ^ step) for i in range(shards)])]
    pallas_call x3 -> x2, Pallas kernels: 20.7 us -> 19 us  [the longest x1 12.4 us: send_first(): pl.pallas_call(functools.partial(send_kernel, groups=groups, shards=shard...]
  transfers between devices with their start and end apart: 12 -> 11, of which waited for: 6 -> 5; matrix products, arithmetic and copies ran while one was open for 3% -> 3% of each run, Pallas kernels for 49% -> 38%
where the time goes in v1:
time: 156 us; the launch traced here: 155 us
  Pallas kernels  77 us (49%)
  waiting for transfers between devices  50.7 us (32%)
  starting transfers between devices  22.2 us (14%)
  local copies, waits for them, and re-layouts  2.97 us (2%)
  other arithmetic  2.16 us (1%)
    pallas_call x2, Pallas kernels, finish_rows(): pl.pallas_call(functools.partial(finish_kernel, start=start, per=per, fol...  37.8 us
    ppermute x3, waiting for transfers between devices, sum_head(): lax.ppermute(value, 'head', [(i, i ^ k) for i in range(groups)])  31.4 us
    pallas_call x1, Pallas kernels, local_sums(): pl.pallas_call(sums_kernel, grid=(local // block,), in_specs=[pl.BlockSpe...  16 us
    all_to_all x2, waiting for transfers between devices, exchange(): lax.all_to_all(rows, ('head', 'pts'), split_axis=0, concat_axis=0, tiled=...  12.8 us
    pallas_call x1, Pallas kernels, send_first(): pl.pallas_call(functools.partial(send_kernel, groups=groups, shards=shard...  12.4 us
    all_to_all x2, starting transfers between devices, exchange(): lax.all_to_all(rows, ('head', 'pts'), split_axis=0, concat_axis=0, tiled=...  10.3 us
    pallas_call x1, Pallas kernels, send_rest(): pl.pallas_call(functools.partial(rest_kernel, first=first), in_specs=[pl....  6.57 us
    ppermute x3, waiting for transfers between devices, sum_plane(): lax.ppermute(value, 'pts', [(i, i ^ step) for i in range(shards)])  6.38 us
  transfers between devices with their start and end apart: 11, of which 5 were waited for; matrix products, arithmetic and copies ran while one was open for 3% of the time, Pallas kernels for 38%

profile of v1, /device:TPU:0, one launch (start us, length us, event | category | flops | bytes accessed | tf_op | source)
XLA Modules:
  0.0 155.4 jit_solution(11567761906653863877)
XLA Ops:
  0.0 4.1 %collective-permute-start.1 = (f32[4]{0:T(128)}, f32[4]{0:T(128)S(1)}, u32[]{:S(2)}, u32[]{:S(2)}) collective-permute-start(f32[4]{0:T(128)} %param.28), channel_id=1, source_target_pairs={{0,16},{8,24},{16,0},{24,8},{1,17},{9,25},{17,1},{25,9},{2,18},{10... | collective-permute-start | bytes 56 | tf_op jit(solution)/shard_map/ppermute | solution.py:534
  4.1 1.6 %collective-permute-start = (f32[4]{0:T(128)}, f32[4]{0:T(128)S(1)}, u32[]{:S(2)}, u32[]{:S(2)}) collective-permute-start(f32[4]{0:T(128)} %param.28), channel_id=1, source_target_pairs={{0,8},{8,0},{16,24},{24,16},{1,9},{9,1},{17,25},{25,17},{2,10},{10... | collective-permute-start | bytes 56 | tf_op jit(solution)/shard_map/ppermute | solution.py:534
  5.6 12.4 %send_first.1 = (s32[32,256]{1,0:T(8,128)}, bf16[32,120,256]{2,1,0:T(8,128)(2,1)}) custom-call(s32[48,128]{1,0:T(8,128)} %bitcast.16, bf16[6144,256]{1,0:T(8,128)(2,1)} %x_ref.3), custom_call_target="tpu_custom_call" | custom-call | tf_op jit(solution)/shard_map/send_first/pallas_call | solution.py:151
  18.1 6.3 %all-to-all-start = ((bf16[32,120,256]{2,1,0:T(8,128)(2,1)}), bf16[32,120,256]{2,1,0:T(8,128)(2,1)S(1)}, u32[]{:S(2)}, u32[]{:S(2)}) async-start(bf16[32,120,256]{2,1,0:T(8,128)(2,1)} %get-tuple-element.20), calls=%async_computation | async-start | bytes 3932160 | tf_op jit(solution)/shard_map/all_to_all | solution.py:531
  24.4 0.8 copy.27
  25.3 0.7 reshape.127.sharp_ref
  26.0 16.0 %local_sums.1 = (f32[32,384]{1,0:T(8,128)}, bf16[512,256]{1,0:T(8,128)(2,1)}) custom-call(bf16[6144,256]{1,0:T(8,128)(2,1)} %x_ref.3, f32[1,256]{1,0:T(1,128)} %bitcast.19, f32[1,256]{1,0:T(1,128)} %bitcast.22, bf16[256,256]{1,0:T(8,128)(2,1)} %attribute.1, bf16[256,256]{1,0:T(8,128)(2,1)} %bitcast.13, bf16[16,32]{1,0:T(8,128)(2,1)} %partition.1, ...), custom_call_target="tpu_custom_call" | custom-call | flops 5000000000 | bytes 4000000 | tf_op jit(solution)/shard_map/local_sums/pallas_call | solution.py:287
  42.1 1.4 collective-permute-done.3
  43.4 0.8 add.22
  44.2 1.6 %collective-permute-start.4 = (f32[32,384]{1,0:T(8,128)S(1)}, f32[32,384]{1,0:T(8,128)S(1)}, u32[]{:S(2)}, u32[]{:S(2)}) collective-permute-start(f32[32,384]{1,0:T(8,128)S(1)} %add.22), channel_id=1, source_target_pairs={{0,2},{1,3},{2,0},{3,1},{4,6},{5,7},{6,4},{7,5},{8,10},{9,11},{10,... | collective-permute-start | bytes 147464 | tf_op jit(solution)/shard_map/ppermute | solution.py:485
  45.8 5.0 %collective-permute-done.4 = f32[32,384]{1,0:T(8,128)S(1)} collective-permute-done((f32[32,384]{1,0:T(8,128)S(1)}, f32[32,384]{1,0:T(8,128)S(1)}, u32[]{:S(2)}, u32[]{:S(2)}) %collective-permute-start.4) | collective-permute-done | bytes 49184 | tf_op jit(solution)/shard_map/ppermute | solution.py:485
  50.9 6.6 %send_rest.1 = bf16[32,80,256]{2,1,0:T(8,128)(2,1)} custom-call(s32[32,256]{1,0:T(8,128)} %get-tuple-element.21.list_ref, bf16[6144,256]{1,0:T(8,128)(2,1)} %x_ref.3), custom_call_target="tpu_custom_call" | custom-call | flops 5120000000 | bytes 6000000 | tf_op jit(solution)/shard_map/send_rest/pallas_call | solution.py:185
  57.5 12.8 %all-to-all-done.x_ref = bf16[32,120,256]{2,1,0:T(8,128)(2,1)S(1)} async-done(((bf16[32,120,256]{2,1,0:T(8,128)(2,1)}), bf16[32,120,256]{2,1,0:T(8,128)(2,1)S(1)}, u32[]{:S(2)}, u32[]{:S(2)}) %all-to-all-start) | async-done | bytes 1966112 | tf_op jit(solution)/shard_map/all_to_all | solution.py:531
  70.4 4.1 %all-to-all-start.1 = ((bf16[32,80,256]{2,1,0:T(8,128)(2,1)}), bf16[32,80,256]{2,1,0:T(8,128)(2,1)S(1)}, u32[]{:S(2)}, u32[]{:S(2)}) async-start(bf16[32,80,256]{2,1,0:T(8,128)(2,1)} %send_rest.1), calls=%async_computation.1 | async-start | bytes 2621440 | tf_op jit(solution)/shard_map/all_to_all | solution.py:531
  74.5 3.5 %collective-permute-start.8 = (f32[32,384]{1,0:T(8,128)S(1)}, f32[32,384]{1,0:T(8,128)S(1)}, u32[]{:S(2)}, u32[]{:S(2)}) collective-permute-start(f32[32,384]{1,0:T(8,128)S(1)} %add.24), channel_id=1, source_target_pairs={{0,24},{8,16},{16,8},{24,0},{1,25},{9,17},{17,9},{25,1},{2,26},{10... | collective-permute-start | bytes 147464 | tf_op jit(solution)/shard_map/ppermute | solution.py:491
  77.9 1.0 collective-permute-start.6
  78.9 22.7 %collective-permute-done.8 = f32[32,384]{1,0:T(8,128)S(1)} collective-permute-done((f32[32,384]{1,0:T(8,128)S(1)}, f32[32,384]{1,0:T(8,128)S(1)}, u32[]{:S(2)}, u32[]{:S(2)}) %collective-permute-start.8) | collective-permute-done | bytes 49184 | tf_op jit(solution)/shard_map/ppermute | solution.py:491
  101.6 8.7 %collective-permute-done.7 = f32[32,384]{1,0:T(8,128)S(1)} collective-permute-done((f32[32,384]{1,0:T(8,128)S(1)}, f32[32,384]{1,0:T(8,128)S(1)}, u32[]{:S(2)}, u32[]{:S(2)}) %collective-permute-start.7) | collective-permute-done | bytes 49184 | tf_op jit(solution)/shard_map/ppermute | solution.py:491
  110.4 0.6 add_add_fusion.packed_ref
  111.0 4.2 %slice_attention.1.mix_t = bf16[256,512]{1,0:T(8,128)(2,1)} custom-call(f32[32,384]{1,0:T(8,128)} %add_add_fusion.packed_ref, f32[16,16]{1,0:T(8,128)} %question.1, f32[16,16]{1,0:T(8,128)} %lookup.1, f32[16,16]{1,0:T(8,128)} %content.1), custom_call_target="tpu_custom_call" | custom-call | tf_op jit(solution)/shard_map/slice_attention/pallas_call | solution.py:352
  115.7 0.6 fusion.1.pos_hbm
  116.4 20.2 %shard_map.190.refs_0_ = f32[12288,128]{1,0:T(8,128)} custom-call(s32[32,256]{1,0:T(8,128)} %fusion.1.pos_hbm, bf16[32,120,256]{2,1,0:T(8,128)(2,1)} %copy-done, f32[1,256]{1,0:T(1,128)} %bitcast.20, f32[1,256]{1,0:T(1,128)} %bitcast.23, bf16[256,256]{1,0:T(8,128)(2,1)} %bitcast.14, bf16[512,256]{1,0:T(8,128)(2,1)} %get-tuple-element.24.logit_t, ...), custom_call_target="tpu_custom_call" | custom-call | flops 7168000000 | bytes 8000000 | tf_op jit(solution)/shard_map/pallas_call | solution.py:451
  136.6 1.0 copy-done.1
  137.6 17.6 %shard_map.191 = bf16[6144,256]{1,0:T(8,128)(2,1)} custom-call(s32[32,256]{1,0:T(8,128)} %fusion.1.pos_hbm, bf16[32,80,256]{2,1,0:T(8,128)(2,1)} %copy-done.1, f32[1,256]{1,0:T(1,128)} %bitcast.21, f32[1,256]{1,0:T(1,128)} %bitcast.24, bf16[256,256]{1,0:T(8,128)(2,1)} %bitcast.15, bf16[512,256]{1,0:T(8,128)(2,1)} %get-tuple-element.24.logit_t, ...), custom_call_target="tpu_custom_call" | custom-call | flops 5120000000 | bytes 8000000 | tf_op jit(solution)/shard_map/pallas_call | solution.py:451
  (25 shorter events, 0.8 us)
Async XLA Ops:
  0.0 18.1 %collective-permute-start.1 = (f32[4]{0:T(128)}, f32[4]{0:T(128)S(1)}, u32[]{:S(2)}, u32[]{:S(2)}) collective-permute-start(f32[4]{0:T(128)} %param.28), channel_id=1, source_target_pairs={{0,16},{8,24},{16,0},{24,8},{1,17},{9,25},{17,1},{25,9},{2,18},{10... | collective-permute-start | bytes 56 | tf_op jit(solution)/shard_map/ppermute | solution.py:534
  4.1 14.0 %collective-permute-start = (f32[4]{0:T(128)}, f32[4]{0:T(128)S(1)}, u32[]{:S(2)}, u32[]{:S(2)}) collective-permute-start(f32[4]{0:T(128)} %param.28), channel_id=1, source_target_pairs={{0,8},{8,0},{16,24},{24,16},{1,9},{9,1},{17,25},{25,17},{2,10},{10... | collective-permute-start | bytes 56 | tf_op jit(solution)/shard_map/ppermute | solution.py:534
  5.6 12.5 %collective-permute-start.2 = (f32[4]{0:T(128)}, f32[4]{0:T(128)S(1)}, u32[]{:S(2)}, u32[]{:S(2)}) collective-permute-start(f32[4]{0:T(128)} %param.28), channel_id=1, source_target_pairs={{0,24},{8,16},{16,8},{24,0},{1,25},{9,17},{17,9},{25,1},{2,26},{10... | collective-permute-start | bytes 56 | tf_op jit(solution)/shard_map/ppermute | solution.py:534
  18.1 6.3 %copy-start.2 = (bf16[256,256]{1,0:T(8,128)(2,1)S(1)}, bf16[256,256]{1,0:T(8,128)(2,1)}, u32[]{:S(2)}) copy-start(bf16[256,256]{1,0:T(8,128)(2,1)} %param.25) | copy-start | bytes 393220
  18.1 7.1 %copy-start.3 = (f32[4]{0:T(128)S(1)}, f32[4]{0:T(128)}, u32[]{:S(2)}) copy-start(f32[4]{0:T(128)} %param.28) | copy-start | bytes 52
  18.1 52.2 %all-to-all-start = ((bf16[32,120,256]{2,1,0:T(8,128)(2,1)}), bf16[32,120,256]{2,1,0:T(8,128)(2,1)S(1)}, u32[]{:S(2)}, u32[]{:S(2)}) async-start(bf16[32,120,256]{2,1,0:T(8,128)(2,1)} %get-tuple-element.20), calls=%async_computation | async-start | bytes 3932160 | tf_op jit(solution)/shard_map/all_to_all | solution.py:531
  42.0 1.4 collective-permute-start.3
  44.2 6.6 %collective-permute-start.4 = (f32[32,384]{1,0:T(8,128)S(1)}, f32[32,384]{1,0:T(8,128)S(1)}, u32[]{:S(2)}, u32[]{:S(2)}) collective-permute-start(f32[32,384]{1,0:T(8,128)S(1)} %add.22), channel_id=1, source_target_pairs={{0,2},{1,3},{2,0},{3,1},{4,6},{5,7},{6,4},{7,5},{8,10},{9,11},{10,... | collective-permute-start | bytes 147464 | tf_op jit(solution)/shard_map/ppermute | solution.py:485
  50.9 6.7 %collective-permute-start.5 = (f32[32,384]{1,0:T(8,128)S(1)}, f32[32,384]{1,0:T(8,128)S(1)}, u32[]{:S(2)}, u32[]{:S(2)}) collective-permute-start(f32[32,384]{1,0:T(8,128)S(1)} %add.23), channel_id=1, source_target_pairs={{0,4},{1,5},{2,6},{3,7},{4,0},{5,1},{6,2},{7,3},{8,12},{9,13},{10,... | collective-permute-start | bytes 147464 | tf_op jit(solution)/shard_map/ppermute | solution.py:485
  70.4 45.3 %copy-start = (bf16[32,120,256]{2,1,0:T(8,128)(2,1)}, bf16[32,120,256]{2,1,0:T(8,128)(2,1)S(1)}, u32[]{:S(2)}) copy-start(bf16[32,120,256]{2,1,0:T(8,128)(2,1)S(1)} %all-to-all-done.x_ref) | copy-start | bytes 5898244
  70.4 66.2 %all-to-all-start.1 = ((bf16[32,80,256]{2,1,0:T(8,128)(2,1)}), bf16[32,80,256]{2,1,0:T(8,128)(2,1)S(1)}, u32[]{:S(2)}, u32[]{:S(2)}) async-start(bf16[32,80,256]{2,1,0:T(8,128)(2,1)} %send_rest.1), calls=%async_computation.1 | async-start | bytes 2621440 | tf_op jit(solution)/shard_map/all_to_all | solution.py:531
  74.5 27.2 %collective-permute-start.8 = (f32[32,384]{1,0:T(8,128)S(1)}, f32[32,384]{1,0:T(8,128)S(1)}, u32[]{:S(2)}, u32[]{:S(2)}) collective-permute-start(f32[32,384]{1,0:T(8,128)S(1)} %add.24), channel_id=1, source_target_pairs={{0,24},{8,16},{16,8},{24,0},{1,25},{9,17},{17,9},{25,1},{2,26},{10... | collective-permute-start | bytes 147464 | tf_op jit(solution)/shard_map/ppermute | solution.py:491
  77.9 32.4 %collective-permute-start.7 = (f32[32,384]{1,0:T(8,128)S(1)}, f32[32,384]{1,0:T(8,128)S(1)}, u32[]{:S(2)}, u32[]{:S(2)}) collective-permute-start(f32[32,384]{1,0:T(8,128)S(1)} %add.24), channel_id=1, source_target_pairs={{0,16},{8,24},{16,0},{24,8},{1,17},{9,25},{17,1},{25,9},{2,18},{10... | collective-permute-start | bytes 147464 | tf_op jit(solution)/shard_map/ppermute | solution.py:491
  77.9 32.4 %collective-permute-start.6 = (f32[32,384]{1,0:T(8,128)S(1)}, f32[32,384]{1,0:T(8,128)S(1)}, u32[]{:S(2)}, u32[]{:S(2)}) collective-permute-start(f32[32,384]{1,0:T(8,128)S(1)} %add.24), channel_id=1, source_target_pairs={{0,8},{8,0},{16,24},{24,16},{1,9},{9,1},{17,25},{25,17},{2,10},{10... | collective-permute-start | bytes 147464 | tf_op jit(solution)/shard_map/ppermute | solution.py:491
  136.6 1.0 copy-start.1

commit v2 on v1

--- a/solution.py
+++ b/solution.py
@@ -13,6 +13,7 @@
 BF16 = jnp.bfloat16
 LANES = 128
 TAIL = 8
+SUBLANES = 8
 BLOCK = 1024
 EPS_NORM = 1e-05
 LOG2E = math.log2(math.e)
@@ -41,28 +42,22 @@
     return centred * lax.rsqrt(spread + EPS_NORM) * gain + bias
 
 
-def narrow_rows(source, first, other, count):
-    low = source[first : first + count, :].astype(BF16)
-    return low, source[other : other + count, :].astype(BF16)
-
-
-def fetch_rows(lists, start, count, src, dst, stage, out, sem, group):
-    local = src.shape[0] // 2
-    devices = lists.shape[0]
-    copies = []
-    for d in range(devices):
-        base = (d % 2) * 2 * count
-        for j in range(count):
-            row = lists[d, start + j]
-            dst[base + j : base + j + 1, :] = src[pl.ds(row, 1), :]
-            dst[base + count + j : base + count + j + 1, :] = src[pl.ds(row + local, 1), :]
-        stage[d, :count, :LANES], stage[d, :count, LANES:] = narrow_rows(dst, base, base + count, count)
-        if (d + 1) % group == 0:
-            part = pl.ds(d + 1 - group, group)
-            copies.append(pltpu.make_async_copy(stage.at[part], out.at[part], sem.at[d // group]))
-            copies[-1].start()
-    for copy in copies:
-        copy.wait()
+def pick_rows(src, base, rows):
+    sub = lax.broadcasted_iota(jnp.int32, (SUBLANES, LANES), 0)
+    merged = src[pl.ds(rows[0] + (base + SUBLANES), SUBLANES), :]
+    for j in range(1, SUBLANES):
+        merged = jnp.where(sub == j, src[pl.ds(rows[j] + (base + SUBLANES - j), SUBLANES), :], merged)
+    return merged.astype(BF16)
+
+
+def fetch_rows(lists, d, start, counts, src, stages):
+    local = src.shape[0] // 2 - SUBLANES
+    for stage, count in zip(stages, counts):
+        for first in range(0, count, SUBLANES):
+            rows = [lists[d, start + first + j] for j in range(SUBLANES)]
+            stage[d, first : first + SUBLANES, :LANES] = pick_rows(src, 0, rows)
+            stage[d, first : first + SUBLANES, LANES:] = pick_rows(src, local, rows)
+        start += count
 
 
 def widen_rows(x_ref, src):
@@ -70,21 +65,21 @@
 
     def widen(c, carry):
         row = pl.multiple_of(c * LANES, LANES)
-        src[pl.ds(row, LANES), :] = x_ref[pl.ds(row, LANES), :LANES].astype(F32)
-        src[pl.ds(row + local, LANES), :] = x_ref[pl.ds(row, LANES), LANES:].astype(F32)
+        src[pl.ds(row + SUBLANES, LANES), :] = x_ref[pl.ds(row, LANES), :LANES].astype(F32)
+        src[pl.ds(row + (local + SUBLANES), LANES), :] = x_ref[pl.ds(row, LANES), LANES:].astype(F32)
         return carry
 
     lax.fori_loop(0, local // LANES, widen, 0)
 
 
 def send_kernel(
-    place_ref, x_hbm, list_ref, out, hot_ref, count_ref, key_ref, x_ref, src, dst, stage, list_s, sem,
+    place_ref, x_hbm, list_ref, out, hot_ref, count_ref, key_ref, x_ref, src, stage, list_s, sem,
     *, groups, shards, first,
 ):
     devices = groups * shards
     chunks = place_ref.shape[0]
-    padded = list_ref.shape[1]
     local, width = x_ref.shape
+    per = local // devices
     rows_in = pltpu.make_async_copy(x_hbm, x_ref, sem.at[0])
     rows_in.start()
     placement = place_ref[...].astype(F32)
@@ -109,42 +104,56 @@
             hot_ref[:, c * LANES : (c + 1) * LANES], prefix, preferred_element_type=F32
         )
     carry = jnp.zeros((devices, LANES), F32)
-    slots = lax.broadcasted_iota(jnp.int32, (padded, LANES), 0).astype(F32)
+    slots = lax.broadcasted_iota(jnp.int32, (per, LANES), 0).astype(F32).astype(BF16)
     lane = lax.broadcasted_iota(jnp.int32, (1, LANES), 1).astype(F32)
+    zero = jnp.zeros((per, LANES), BF16)
     for c in range(chunks):
         counts = count_ref[c * devices : (c + 1) * devices, :]
         hot = hot_ref[:, c * LANES : (c + 1) * LANES].astype(F32)
         rank = jnp.sum(hot * (counts[:, :LANES] + carry), axis=0, keepdims=True)
         carry = carry + counts[:, LANES:]
-        chosen = slots == rank
-        values = (high[c : c + 1, :], low[c : c + 1, :], float(c), lane)
+        chosen = slots == jnp.broadcast_to(rank, (per, LANES)).astype(BF16)
+        values = (high[c : c + 1, :], low[c : c + 1, :], jnp.full((1, LANES), float(c), F32), lane)
         for k, value in enumerate(values):
-            key_ref[k * padded : (k + 1) * padded, c * LANES : (c + 1) * LANES] = jnp.where(
-                chosen, value, 0.0
-            ).astype(BF16)
+            key_ref[k * per : (k + 1) * per, c * LANES : (c + 1) * LANES] = jnp.where(
+                chosen, jnp.broadcast_to(value, (per, LANES)).astype(BF16), zero
+            )
     codes = lax.dot_general(hot_ref[...], key_ref[...], NT, preferred_element_type=F32)
-    source = codes[:, 2 * padded : 3 * padded] * LANES + codes[:, 3 * padded :]
-    list_ref[...] = source.astype(jnp.int32)
+    source = codes[:, 2 * per : 3 * per] * LANES + codes[:, 3 * per :]
+    list_ref[...] = jnp.zeros_like(list_ref)
+    list_ref[:, :per] = source.astype(jnp.int32)
     lists_in = pltpu.make_async_copy(list_ref, list_s, sem.at[1])
     lists_in.start()
-    line = lax.broadcasted_iota(jnp.int32, (TAIL, padded), 0)
+    line = lax.broadcasted_iota(jnp.int32, (TAIL, per), 0)
+    label_high, label_low = codes[:, :per], codes[:, per : 2 * per]
+    stage[:, first:, :] = jnp.zeros((devices, TAIL, width), BF16)
     for d in range(devices):
-        tail = jnp.where(
-            line == 0, codes[d : d + 1, :padded], jnp.where(line == 1, codes[d : d + 1, padded : 2 * padded], 0.0)
-        )
-        if padded < width:
-            tail = jnp.concatenate([tail, jnp.zeros((TAIL, width - padded), F32)], axis=1)
-        stage[d, first:, :] = tail.astype(BF16)
+        tail = jnp.where(line == 0, label_high[d : d + 1], jnp.where(line == 1, label_low[d : d + 1], 0.0))
+        stage[d, first:, :per] = tail.astype(BF16)
     rows_in.wait()
     widen_rows(x_ref, src)
     lists_in.wait()
-    fetch_rows(list_s, 0, first, src, dst, stage, out, sem, devices // sem.shape[0])
+    copies = []
+    group = devices // sem.shape[0]
+    for g in range(sem.shape[0]):
+
+        def fetch(d, carry):
+            fetch_rows(list_s, d, 0, (first,), src, (stage,))
+            return carry
+
+        lax.fori_loop(g * group, (g + 1) * group, fetch, 0)
+        part = pl.ds(g * group, group)
+        copies.append(pltpu.make_async_copy(stage.at[part], out.at[part], sem.at[g]))
+        copies[-1].start()
+    for copy in copies:
+        copy.wait()
 
 
 def send_first(placement, rows, groups, shards, first):
     devices = groups * shards
     local, width = rows.shape
-    padded = -(-(local // devices) // LANES) * LANES
+    per = local // devices
+    padded = -(-per // LANES) * LANES
     chunks = local // LANES
     vmem = pl.BlockSpec(memory_space=pltpu.VMEM)
     hbm = pl.BlockSpec(memory_space=pl.ANY)
@@ -159,10 +168,9 @@
         scratch_shapes=[
             pltpu.VMEM((devices, local), BF16),
             pltpu.VMEM((chunks * devices, 2 * LANES), F32),
-            pltpu.VMEM((4 * padded, local), BF16),
+            pltpu.VMEM((4 * per, local), BF16),
             pltpu.VMEM((local, width), BF16),
-            pltpu.VMEM((2 * local, LANES), F32),
-            pltpu.VMEM((4 * first, LANES), F32),
+            pltpu.VMEM((2 * (local + SUBLANES), LANES), F32),
             pltpu.VMEM((devices, first + TAIL, width), BF16),
             pltpu.SMEM((devices, padded), jnp.int32),
             pltpu.SemaphoreType.DMA((4,)),
@@ -172,30 +180,27 @@
     )(placement.reshape(chunks, LANES), rows)
 
 
-def rest_kernel(list_ref, x_ref, out, src, dst, stage, sem, *, first):
+def rest_kernel(list_ref, x_ref, one, two, src, *, first):
     widen_rows(x_ref, src)
-    fetch_rows(
-        list_ref, first, out.shape[1], src, dst, stage, out, sem, list_ref.shape[0] // sem.shape[0]
-    )
-
-
-def send_rest(lists, rows, first, count):
+
+    def fetch(d, carry):
+        fetch_rows(list_ref, d, first, (one.shape[1], two.shape[1]), src, (one, two))
+        return carry
+
+    lax.fori_loop(0, list_ref.shape[0], fetch, 0)
+
+
+def send_rest(lists, rows, first, counts):
     local, width = rows.shape
     devices = lists.shape[0]
     return pl.pallas_call(
         functools.partial(rest_kernel, first=first),
         in_specs=[pl.BlockSpec(memory_space=pltpu.SMEM), pl.BlockSpec(memory_space=pltpu.VMEM)],
-        out_specs=pl.BlockSpec(memory_space=pl.ANY),
-        out_shape=jax.ShapeDtypeStruct((devices, count, width), BF16),
-        scratch_shapes=[
-            pltpu.VMEM((2 * local, LANES), F32),
-            pltpu.VMEM((4 * count, LANES), F32),
-            pltpu.VMEM((devices, count, width), BF16),
-            pltpu.SemaphoreType.DMA((4,)),
-        ],
+        out_shape=[jax.ShapeDtypeStruct((devices, n, width), BF16) for n in counts],
+        scratch_shapes=[pltpu.VMEM((2 * (local + SUBLANES), LANES), F32)],
         compiler_params=params(),
         cost_estimate=pl.CostEstimate(
-            flops=2_000_000 * devices * count, bytes_accessed=6_000_000, transcendentals=0
+            flops=2_000_000 * devices * sum(counts), bytes_accessed=6_000_000, transcendentals=0
         ),
         name="send_rest",
     )(lists, rows)
@@ -524,8 +529,9 @@
     heads = width // feature
     per = local // devices
     block = 768 if local % 768 == 0 else LANES
-    first = per * 7 // 12 // 8 * 8
-    second = per - first
+    first = per // 2 // 8 * 8
+    second = per // 3 // 8 * 8
+    third = per - first - second
 
     def exchange(rows):
         return lax.all_to_all(rows, ("head", "pts"), split_axis=0, concat_axis=0, tiled=True)
@@ -537,7 +543,7 @@
     lists, one = send_first(inference_placement, layer_inputs_trainorder, groups, shards, first)
     *mates, one = lax.optimization_barrier((*mates, one))
     arrived_one = exchange(one)
-    two = send_rest(lists, layer_inputs_trainorder, first, second)
+    two, three = send_rest(lists, layer_inputs_trainorder, first, (second, third))
 
     place = lax.axis_index("head")
     order = jnp.arange(groups)[:, None]
@@ -572,8 +578,13 @@
     served = finish_rows(
         arrived_at, arrived_one, weights, offset, mix_t, rest, None, local, 0, first, False
     )
+    served, arrived_two, three = lax.optimization_barrier((served, arrived_two, three))
+    arrived_three = exchange(three)
     served = finish_rows(
-        arrived_at, arrived_two, weights, offset, mix_t, rest, served, local, first, second, True
+        arrived_at, arrived_two, weights, offset, mix_t, rest, served, local, first, second, False
+    )
+    served = finish_rows(
+        arrived_at, arrived_three, weights, offset, mix_t, rest, served, local, first + second, third, True
     )
     return served[None]
 

time: 156 us -> 152 us (0.974)
  waiting for transfers between devices: 50.7 us -> 38 us
  starting transfers between devices: 22.2 us -> 27.8 us
  Pallas kernels: 77 us -> 80.2 us
    ppermute x3, waiting for transfers between devices: 31.4 us -> 25.8 us  [sum_head(): lax.ppermute(value, 'head', [(i, i ^ k) for i in range(groups)])]
    pallas_call x2 -> x3, Pallas kernels: 37.8 us -> 42.3 us  [finish_rows(): pl.pallas_call(functools.partial(finish_kernel, start=start, per=per, fol...]
    all_to_all x2 -> x3, waiting for transfers between devices: 12.8 us -> 8.53 us  [exchange(): lax.all_to_all(rows, ('head', 'pts'), split_axis=0, concat_axis=0, tiled=...]
    all_to_all x2 -> x3, starting transfers between devices: 10.3 us -> 14 us  [exchange(): lax.all_to_all(rows, ('head', 'pts'), split_axis=0, concat_axis=0, tiled=...]
    ppermute x3, waiting for transfers between devices: 6.38 us -> 3.69 us  [sum_plane(): lax.ppermute(value, 'pts', [(i, i ^ step) for i in range(shards)])]
    pallas_call x1, Pallas kernels: 12.4 us -> 10.5 us  [send_first(): pl.pallas_call(functools.partial(send_kernel, groups=groups, shards=shard...]
    ppermute x3, starting transfers between devices: 1.75 us -> 3.67 us  [sum_plane(): lax.ppermute(value, 'pts', [(i, i ^ step) for i in range(shards)])]
  transfers between devices with their start and end apart: 11 -> 12, of which waited for: 5 -> 6; matrix products, arithmetic and copies ran while one was open for 3% -> 3% of each run, Pallas kernels for 38% -> 47%
where the time goes in v2:
time: 152 us; the launch traced here: 151 us
  Pallas kernels  80.2 us (53%)
  waiting for transfers between devices  38 us (25%)
  starting transfers between devices  27.8 us (18%)
  local copies, waits for them, and re-layouts  2.66 us (2%)
  other arithmetic  2.17 us (1%)
    pallas_call x3, Pallas kernels, finish_rows(): pl.pallas_call(functools.partial(finish_kernel, start=start, per=per, fol...  42.3 us
    ppermute x3, waiting for transfers between devices, sum_head(): lax.ppermute(value, 'head', [(i, i ^ k) for i in range(groups)])  25.8 us
    pallas_call x1, Pallas kernels, local_sums(): pl.pallas_call(sums_kernel, grid=(local // block,), in_specs=[pl.BlockSpe...  16 us
    all_to_all x3, starting transfers between devices, exchange(): lax.all_to_all(rows, ('head', 'pts'), split_axis=0, concat_axis=0, tiled=...  14 us
    pallas_call x1, Pallas kernels, send_first(): pl.pallas_call(functools.partial(send_kernel, groups=groups, shards=shard...  10.5 us
    all_to_all x3, waiting for transfers between devices, exchange(): lax.all_to_all(rows, ('head', 'pts'), split_axis=0, concat_axis=0, tiled=...  8.53 us
    pallas_call x1, Pallas kernels, send_rest(): pl.pallas_call(functools.partial(rest_kernel, first=first), in_specs=[pl....  7.27 us
    ppermute x3, starting transfers between devices, body(): lax.ppermute(softmax_sharpness, 'head', [(i, i ^ k) for i in range(groups)])  5.64 us
  transfers between devices with their start and end apart: 12, of which 6 were waited for; matrix products, arithmetic and copies ran while one was open for 3% of the time, Pallas kernels for 47%

profile of v2, /device:TPU:0, one launch (start us, length us, event | category | flops | bytes accessed | tf_op | source)
XLA Modules:
  0.0 151.2 jit_solution(3595820968184539869)
XLA Ops:
  0.0 4.1 %collective-permute-start.1 = (f32[4]{0:T(128)}, f32[4]{0:T(128)S(1)}, u32[]{:S(2)}, u32[]{:S(2)}) collective-permute-start(f32[4]{0:T(128)} %param.28), channel_id=1, source_target_pairs={{0,16},{8,24},{16,0},{24,8},{1,17},{9,25},{17,1},{25,9},{2,18},{10... | collective-permute-start | bytes 56 | tf_op jit(solution)/shard_map/ppermute | solution.py:540
  4.1 1.6 %collective-permute-start = (f32[4]{0:T(128)}, f32[4]{0:T(128)S(1)}, u32[]{:S(2)}, u32[]{:S(2)}) collective-permute-start(f32[4]{0:T(128)} %param.28), channel_id=1, source_target_pairs={{0,8},{8,0},{16,24},{24,16},{1,9},{9,1},{17,25},{25,17},{2,10},{10... | collective-permute-start | bytes 56 | tf_op jit(solution)/shard_map/ppermute | solution.py:540
  5.7 10.5 %send_first.1 = (s32[32,256]{1,0:T(8,128)}, bf16[32,104,256]{2,1,0:T(8,128)(2,1)}) custom-call(s32[48,128]{1,0:T(8,128)} %bitcast.17, bf16[6144,256]{1,0:T(8,128)(2,1)} %x_ref.3), custom_call_target="tpu_custom_call" | custom-call | tf_op jit(solution)/shard_map/send_first/pallas_call | solution.py:160
  16.2 6.1 %all-to-all-start = ((bf16[32,104,256]{2,1,0:T(8,128)(2,1)}), bf16[32,104,256]{2,1,0:T(8,128)(2,1)S(1)}, u32[]{:S(2)}, u32[]{:S(2)}) async-start(bf16[32,104,256]{2,1,0:T(8,128)(2,1)} %get-tuple-element.25), calls=%async_computation | async-start | bytes 3407872 | tf_op jit(solution)/shard_map/all_to_all | solution.py:537
  23.8 16.0 %local_sums.1 = (f32[32,384]{1,0:T(8,128)}, bf16[512,256]{1,0:T(8,128)(2,1)}) custom-call(bf16[6144,256]{1,0:T(8,128)(2,1)} %x_ref.3, f32[1,256]{1,0:T(1,128)} %bitcast.21, f32[1,256]{1,0:T(1,128)} %bitcast.25, bf16[256,256]{1,0:T(8,128)(2,1)} %attribute.1, bf16[256,256]{1,0:T(8,128)(2,1)} %bitcast.13, bf16[16,32]{1,0:T(8,128)(2,1)} %partition.1, ...), custom_call_target="tpu_custom_call" | custom-call | flops 5000000000 | bytes 4000000 | tf_op jit(solution)/shard_map/local_sums/pallas_call | solution.py:292
  40.1 1.2 collective-permute-done.3
  41.3 0.8 add.22
  42.1 1.8 %collective-permute-start.4 = (f32[32,384]{1,0:T(8,128)S(1)}, f32[32,384]{1,0:T(8,128)S(1)}, u32[]{:S(2)}, u32[]{:S(2)}) collective-permute-start(f32[32,384]{1,0:T(8,128)S(1)} %add.22), channel_id=1, source_target_pairs={{0,2},{1,3},{2,0},{3,1},{4,6},{5,7},{6,4},{7,5},{8,10},{9,11},{10,... | collective-permute-start | bytes 147464 | tf_op jit(solution)/shard_map/ppermute | solution.py:490
  43.8 2.5 %collective-permute-done.4 = f32[32,384]{1,0:T(8,128)S(1)} collective-permute-done((f32[32,384]{1,0:T(8,128)S(1)}, f32[32,384]{1,0:T(8,128)S(1)}, u32[]{:S(2)}, u32[]{:S(2)}) %collective-permute-start.4) | collective-permute-done | bytes 49184 | tf_op jit(solution)/shard_map/ppermute | solution.py:490
  46.3 1.7 %collective-permute-start.5 = (f32[32,384]{1,0:T(8,128)S(1)}, f32[32,384]{1,0:T(8,128)S(1)}, u32[]{:S(2)}, u32[]{:S(2)}) collective-permute-start(f32[32,384]{1,0:T(8,128)S(1)} %add.23), channel_id=1, source_target_pairs={{0,4},{1,5},{2,6},{3,7},{4,0},{5,1},{6,2},{7,3},{8,12},{9,13},{10,... | collective-permute-start | bytes 147464 | tf_op jit(solution)/shard_map/ppermute | solution.py:490
  48.0 7.3 %send_rest.1 = (bf16[32,64,256]{2,1,0:T(8,128)(2,1)}, bf16[32,32,256]{2,1,0:T(8,128)(2,1)}) custom-call(s32[32,256]{1,0:T(8,128)} %get-tuple-element.26.list_ref, bf16[6144,256]{1,0:T(8,128)(2,1)} %x_ref.3), custom_call_target="tpu_custom_call" | custom-call | flops 6144000000 | bytes 6000000 | tf_op jit(solution)/shard_map/send_rest/pallas_call | solution.py:196
  55.3 7.4 %all-to-all-done.x_ref = bf16[32,104,256]{2,1,0:T(8,128)(2,1)S(1)} async-done(((bf16[32,104,256]{2,1,0:T(8,128)(2,1)}), bf16[32,104,256]{2,1,0:T(8,128)(2,1)S(1)}, u32[]{:S(2)}, u32[]{:S(2)}) %all-to-all-start) | async-done | bytes 1703968 | tf_op jit(solution)/shard_map/all_to_all | solution.py:537
  62.7 4.1 %all-to-all-start.1 = ((bf16[32,64,256]{2,1,0:T(8,128)(2,1)}), bf16[32,64,256]{2,1,0:T(8,128)(2,1)S(1)}, u32[]{:S(2)}, u32[]{:S(2)}) async-start(bf16[32,64,256]{2,1,0:T(8,128)(2,1)} %get-tuple-element.30), calls=%async_computation.1 | async-start | bytes 2097152 | tf_op jit(solution)/shard_map/all_to_all | solution.py:537
  66.8 3.5 %collective-permute-start.8 = (f32[32,384]{1,0:T(8,128)S(1)}, f32[32,384]{1,0:T(8,128)S(1)}, u32[]{:S(2)}, u32[]{:S(2)}) collective-permute-start(f32[32,384]{1,0:T(8,128)S(1)} %add.24), channel_id=1, source_target_pairs={{0,24},{8,16},{16,8},{24,0},{1,25},{9,17},{17,9},{25,1},{2,26},{10... | collective-permute-start | bytes 147464 | tf_op jit(solution)/shard_map/ppermute | solution.py:496
  70.3 0.9 collective-permute-start.6
  71.2 18.5 %collective-permute-done.8 = f32[32,384]{1,0:T(8,128)S(1)} collective-permute-done((f32[32,384]{1,0:T(8,128)S(1)}, f32[32,384]{1,0:T(8,128)S(1)}, u32[]{:S(2)}, u32[]{:S(2)}) %collective-permute-start.8) | collective-permute-done | bytes 49184 | tf_op jit(solution)/shard_map/ppermute | solution.py:496
  89.8 7.3 %collective-permute-done.7 = f32[32,384]{1,0:T(8,128)S(1)} collective-permute-done((f32[32,384]{1,0:T(8,128)S(1)}, f32[32,384]{1,0:T(8,128)S(1)}, u32[]{:S(2)}, u32[]{:S(2)}) %collective-permute-start.7) | collective-permute-done | bytes 49184 | tf_op jit(solution)/shard_map/ppermute | solution.py:496
  97.6 4.2 %slice_attention.1.mix_t = bf16[256,512]{1,0:T(8,128)(2,1)} custom-call(f32[32,384]{1,0:T(8,128)} %add_add_fusion.packed_ref, f32[16,16]{1,0:T(8,128)} %question.1, f32[16,16]{1,0:T(8,128)} %lookup.1, f32[16,16]{1,0:T(8,128)} %content.1), custom_call_target="tpu_custom_call" | custom-call | tf_op jit(solution)/shard_map/slice_attention/pallas_call | solution.py:357
  102.9 19.6 %shard_map.190.refs_0_ = f32[12288,128]{1,0:T(8,128)} custom-call(s32[32,256]{1,0:T(8,128)} %fusion.1.pos_hbm, bf16[32,104,256]{2,1,0:T(8,128)(2,1)} %copy-done, f32[1,256]{1,0:T(1,128)} %bitcast.22, f32[1,256]{1,0:T(1,128)} %bitcast.26, bf16[256,256]{1,0:T(8,128)(2,1)} %bitcast.14, bf16[512,256]{1,0:T(8,128)(2,1)} %get-tuple-element.29.logit_t, ...), custom_call_target="tpu_custom_call" | custom-call | flops 6144000000 | bytes 8000000 | tf_op jit(solution)/shard_map/pallas_call | solution.py:456
  122.5 3.8 %all-to-all-start.2 = ((bf16[32,32,256]{2,1,0:T(8,128)(2,1)}), bf16[32,32,256]{2,1,0:T(8,128)(2,1)S(1)}, u32[]{:S(2)}, u32[]{:S(2)}) async-start(bf16[32,32,256]{2,1,0:T(8,128)(2,1)} %get-tuple-element.32), calls=%async_computation.2 | async-start | bytes 1048576 | tf_op jit(solution)/shard_map/all_to_all | solution.py:537
  126.4 14.2 %shard_map.191.refs_0_ = f32[12288,128]{1,0:T(8,128)} custom-call(s32[32,256]{1,0:T(8,128)} %fusion.1.pos_hbm, bf16[32,64,256]{2,1,0:T(8,128)(2,1)} %copy-done.1, f32[1,256]{1,0:T(1,128)} %bitcast.23, f32[1,256]{1,0:T(1,128)} %bitcast.27, bf16[256,256]{1,0:T(8,128)(2,1)} %bitcast.15, bf16[512,256]{1,0:T(8,128)(2,1)} %get-tuple-element.29.logit_t, ...), custom_call_target="tpu_custom_call" | custom-call | flops 4096000000 | bytes 8000000 | tf_op jit(solution)/shard_map/pallas_call | solution.py:456
  140.6 1.1 all-to-all-done.2.x_ref
  141.8 0.8 copy-done.2
  142.6 8.5 %shard_map.192 = bf16[6144,256]{1,0:T(8,128)(2,1)} custom-call(s32[32,256]{1,0:T(8,128)} %fusion.1.pos_hbm, bf16[32,32,256]{2,1,0:T(8,128)(2,1)} %copy-done.2, f32[1,256]{1,0:T(1,128)} %bitcast.24, f32[1,256]{1,0:T(1,128)} %bitcast.28, bf16[256,256]{1,0:T(8,128)(2,1)} %bitcast.16, bf16[512,256]{1,0:T(8,128)(2,1)} %get-tuple-element.29.logit_t, ...), custom_call_target="tpu_custom_call" | custom-call | flops 2048000000 | bytes 8000000 | tf_op jit(solution)/shard_map/pallas_call | solution.py:456
  (30 shorter events, 3.5 us)
Async XLA Ops:
  0.0 16.1 %collective-permute-start.1 = (f32[4]{0:T(128)}, f32[4]{0:T(128)S(1)}, u32[]{:S(2)}, u32[]{:S(2)}) collective-permute-start(f32[4]{0:T(128)} %param.28), channel_id=1, source_target_pairs={{0,16},{8,24},{16,0},{24,8},{1,17},{9,25},{17,1},{25,9},{2,18},{10... | collective-permute-start | bytes 56 | tf_op jit(solution)/shard_map/ppermute | solution.py:540
  4.1 12.1 %collective-permute-start = (f32[4]{0:T(128)}, f32[4]{0:T(128)S(1)}, u32[]{:S(2)}, u32[]{:S(2)}) collective-permute-start(f32[4]{0:T(128)} %param.28), channel_id=1, source_target_pairs={{0,8},{8,0},{16,24},{24,16},{1,9},{9,1},{17,25},{25,17},{2,10},{10... | collective-permute-start | bytes 56 | tf_op jit(solution)/shard_map/ppermute | solution.py:540
  5.6 10.5 %collective-permute-start.2 = (f32[4]{0:T(128)}, f32[4]{0:T(128)S(1)}, u32[]{:S(2)}, u32[]{:S(2)}) collective-permute-start(f32[4]{0:T(128)} %param.28), channel_id=1, source_target_pairs={{0,24},{8,16},{16,8},{24,0},{1,25},{9,17},{17,9},{25,1},{2,26},{10... | collective-permute-start | bytes 56 | tf_op jit(solution)/shard_map/ppermute | solution.py:540
  5.6 16.6 %copy-start.3 = (bf16[256,256]{1,0:T(8,128)(2,1)S(1)}, bf16[256,256]{1,0:T(8,128)(2,1)}, u32[]{:S(2)}) copy-start(bf16[256,256]{1,0:T(8,128)(2,1)} %param.25) | copy-start | bytes 393220
  5.6 17.4 %copy-start.4 = (f32[4]{0:T(128)S(1)}, f32[4]{0:T(128)}, u32[]{:S(2)}) copy-start(f32[4]{0:T(128)} %param.28) | copy-start | bytes 52
  16.2 46.5 %all-to-all-start = ((bf16[32,104,256]{2,1,0:T(8,128)(2,1)}), bf16[32,104,256]{2,1,0:T(8,128)(2,1)S(1)}, u32[]{:S(2)}, u32[]{:S(2)}) async-start(bf16[32,104,256]{2,1,0:T(8,128)(2,1)} %get-tuple-element.25), calls=%async_computation | async-start | bytes 3407872 | tf_op jit(solution)/shard_map/all_to_all | solution.py:537
  39.8 1.4 collective-permute-start.3
  42.1 4.3 %collective-permute-start.4 = (f32[32,384]{1,0:T(8,128)S(1)}, f32[32,384]{1,0:T(8,128)S(1)}, u32[]{:S(2)}, u32[]{:S(2)}) collective-permute-start(f32[32,384]{1,0:T(8,128)S(1)} %add.22), channel_id=1, source_target_pairs={{0,2},{1,3},{2,0},{3,1},{4,6},{5,7},{6,4},{7,5},{8,10},{9,11},{10,... | collective-permute-start | bytes 147464 | tf_op jit(solution)/shard_map/ppermute | solution.py:490
  46.3 8.9 %collective-permute-start.5 = (f32[32,384]{1,0:T(8,128)S(1)}, f32[32,384]{1,0:T(8,128)S(1)}, u32[]{:S(2)}, u32[]{:S(2)}) collective-permute-start(f32[32,384]{1,0:T(8,128)S(1)} %add.23), channel_id=1, source_target_pairs={{0,4},{1,5},{2,6},{3,7},{4,0},{5,1},{6,2},{7,3},{8,12},{9,13},{10,... | collective-permute-start | bytes 147464 | tf_op jit(solution)/shard_map/ppermute | solution.py:490
  62.7 39.6 %copy-start = (bf16[32,104,256]{2,1,0:T(8,128)(2,1)}, bf16[32,104,256]{2,1,0:T(8,128)(2,1)S(1)}, u32[]{:S(2)}) copy-start(bf16[32,104,256]{2,1,0:T(8,128)(2,1)S(1)} %all-to-all-done.x_ref) | copy-start | bytes 5111812
  62.7 59.8 %all-to-all-start.1 = ((bf16[32,64,256]{2,1,0:T(8,128)(2,1)}), bf16[32,64,256]{2,1,0:T(8,128)(2,1)S(1)}, u32[]{:S(2)}, u32[]{:S(2)}) async-start(bf16[32,64,256]{2,1,0:T(8,128)(2,1)} %get-tuple-element.30), calls=%async_computation.1 | async-start | bytes 2097152 | tf_op jit(solution)/shard_map/all_to_all | solution.py:537
  66.8 23.0 %collective-permute-start.8 = (f32[32,384]{1,0:T(8,128)S(1)}, f32[32,384]{1,0:T(8,128)S(1)}, u32[]{:S(2)}, u32[]{:S(2)}) collective-permute-start(f32[32,384]{1,0:T(8,128)S(1)} %add.24), channel_id=1, source_target_pairs={{0,24},{8,16},{16,8},{24,0},{1,25},{9,17},{17,9},{25,1},{2,26},{10... | collective-permute-start | bytes 147464 | tf_op jit(solution)/shard_map/ppermute | solution.py:496
  70.3 26.7 %collective-permute-start.7 = (f32[32,384]{1,0:T(8,128)S(1)}, f32[32,384]{1,0:T(8,128)S(1)}, u32[]{:S(2)}, u32[]{:S(2)}) collective-permute-start(f32[32,384]{1,0:T(8,128)S(1)} %add.24), channel_id=1, source_target_pairs={{0,16},{8,24},{16,0},{24,8},{1,17},{9,25},{17,1},{25,9},{2,18},{10... | collective-permute-start | bytes 147464 | tf_op jit(solution)/shard_map/ppermute | solution.py:496
  70.3 26.7 %collective-permute-start.6 = (f32[32,384]{1,0:T(8,128)S(1)}, f32[32,384]{1,0:T(8,128)S(1)}, u32[]{:S(2)}, u32[]{:S(2)}) collective-permute-start(f32[32,384]{1,0:T(8,128)S(1)} %add.24), channel_id=1, source_target_pairs={{0,8},{8,0},{16,24},{24,16},{1,9},{9,1},{17,25},{25,17},{2,10},{10... | collective-permute-start | bytes 147464 | tf_op jit(solution)/shard_map/ppermute | solution.py:496
  122.5 3.9 %copy-start.1 = (bf16[32,64,256]{2,1,0:T(8,128)(2,1)}, bf16[32,64,256]{2,1,0:T(8,128)(2,1)S(1)}, u32[]{:S(2)}) copy-start(bf16[32,64,256]{2,1,0:T(8,128)(2,1)S(1)} %all-to-all-done.1.x_ref) | copy-start | bytes 3145732
  122.5 19.2 %all-to-all-start.2 = ((bf16[32,32,256]{2,1,0:T(8,128)(2,1)}), bf16[32,32,256]{2,1,0:T(8,128)(2,1)S(1)}, u32[]{:S(2)}, u32[]{:S(2)}) async-start(bf16[32,32,256]{2,1,0:T(8,128)(2,1)} %get-tuple-element.32), calls=%async_computation.2 | async-start | bytes 1048576 | tf_op jit(solution)/shard_map/all_to_all | solution.py:537
  141.8 0.8 copy-start.2

commit v3 on v2

--- a/solution.py
+++ b/solution.py
@@ -42,22 +42,27 @@
     return centred * lax.rsqrt(spread + EPS_NORM) * gain + bias
 
 
-def pick_rows(src, base, rows):
-    sub = lax.broadcasted_iota(jnp.int32, (SUBLANES, LANES), 0)
-    merged = src[pl.ds(rows[0] + (base + SUBLANES), SUBLANES), :]
-    for j in range(1, SUBLANES):
-        merged = jnp.where(sub == j, src[pl.ds(rows[j] + (base + SUBLANES - j), SUBLANES), :], merged)
-    return merged.astype(BF16)
-
-
-def fetch_rows(lists, d, start, counts, src, stages):
-    local = src.shape[0] // 2 - SUBLANES
+def pick_rows(src, places):
+    pair = lax.broadcasted_iota(jnp.int32, (SUBLANES, LANES), 0) // 2
+    merged = src[pl.ds(places[0] + SUBLANES, SUBLANES), :]
+    for j in range(1, len(places)):
+        merged = jnp.where(pair == j, src[pl.ds(places[j] + (SUBLANES - 2 * j), SUBLANES), :], merged)
+    return merged
+
+
+def fetch_rows(lists, d, start, counts, src, mix, stages):
+    half = SUBLANES // 2
+    done = 0
+    for count in counts:
+        for first in range(done, done + count, half):
+            places = [lists[d, start + first + j] for j in range(half)]
+            mix[2 * first : 2 * first + SUBLANES, :] = pick_rows(src, places)
+        done += count
+    done = 0
     for stage, count in zip(stages, counts):
-        for first in range(0, count, SUBLANES):
-            rows = [lists[d, start + first + j] for j in range(SUBLANES)]
-            stage[d, first : first + SUBLANES, :LANES] = pick_rows(src, 0, rows)
-            stage[d, first : first + SUBLANES, LANES:] = pick_rows(src, local, rows)
-        start += count
+        stage[d, :count, :LANES] = mix[pl.ds(2 * done, count, stride=2), :].astype(BF16)
+        stage[d, :count, LANES:] = mix[pl.ds(2 * done + 1, count, stride=2), :].astype(BF16)
+        done += count
 
 
 def widen_rows(x_ref, src):
@@ -65,15 +70,16 @@
 
     def widen(c, carry):
         row = pl.multiple_of(c * LANES, LANES)
-        src[pl.ds(row + SUBLANES, LANES), :] = x_ref[pl.ds(row, LANES), :LANES].astype(F32)
-        src[pl.ds(row + (local + SUBLANES), LANES), :] = x_ref[pl.ds(row, LANES), LANES:].astype(F32)
+        place = pl.multiple_of(2 * row + SUBLANES, SUBLANES)
+        src[pl.ds(place, LANES, stride=2), :] = x_ref[pl.ds(row, LANES), :LANES].astype(F32)
+        src[pl.ds(place + 1, LANES, stride=2), :] = x_ref[pl.ds(row, LANES), LANES:].astype(F32)
         return carry
 
     lax.fori_loop(0, local // LANES, widen, 0)
 
 
 def send_kernel(
-    place_ref, x_hbm, list_ref, out, hot_ref, count_ref, key_ref, x_ref, src, stage, list_s, sem,
+    place_ref, x_hbm, list_ref, out, hot_ref, count_ref, key_ref, x_ref, src, mix, stage, list_s, sem,
     *, groups, shards, first,
 ):
     devices = groups * shards
@@ -104,6 +110,9 @@
             hot_ref[:, c * LANES : (c + 1) * LANES], prefix, preferred_element_type=F32
         )
     carry = jnp.zeros((devices, LANES), F32)
+    wide = list_ref.shape[1] // LANES
+    order = lax.broadcasted_iota(jnp.int32, (devices, wide * LANES), 1).astype(F32)
+    passed = jnp.zeros((devices, wide * LANES), F32)
     slots = lax.broadcasted_iota(jnp.int32, (per, LANES), 0).astype(F32).astype(BF16)
     lane = lax.broadcasted_iota(jnp.int32, (1, LANES), 1).astype(F32)
     zero = jnp.zeros((per, LANES), BF16)
@@ -112,14 +121,15 @@
         hot = hot_ref[:, c * LANES : (c + 1) * LANES].astype(F32)
         rank = jnp.sum(hot * (counts[:, :LANES] + carry), axis=0, keepdims=True)
         carry = carry + counts[:, LANES:]
+        passed = passed + (jnp.concatenate([carry] * wide, axis=1) <= order).astype(F32)
         chosen = slots == jnp.broadcast_to(rank, (per, LANES)).astype(BF16)
-        values = (high[c : c + 1, :], low[c : c + 1, :], jnp.full((1, LANES), float(c), F32), lane)
+        values = (high[c : c + 1, :], low[c : c + 1, :], lane)
         for k, value in enumerate(values):
             key_ref[k * per : (k + 1) * per, c * LANES : (c + 1) * LANES] = jnp.where(
                 chosen, jnp.broadcast_to(value, (per, LANES)).astype(BF16), zero
             )
     codes = lax.dot_general(hot_ref[...], key_ref[...], NT, preferred_element_type=F32)
-    source = codes[:, 2 * per : 3 * per] * LANES + codes[:, 3 * per :]
+    source = 2.0 * (passed[:, :per] * LANES + codes[:, 2 * per :])
     list_ref[...] = jnp.zeros_like(list_ref)
     list_ref[:, :per] = source.astype(jnp.int32)
     lists_in = pltpu.make_async_copy(list_ref, list_s, sem.at[1])
@@ -136,12 +146,9 @@
     copies = []
     group = devices // sem.shape[0]
     for g in range(sem.shape[0]):
-
-        def fetch(d, carry):
-            fetch_rows(list_s, d, 0, (first,), src, (stage,))
-            return carry
-
-        lax.fori_loop(g * group, (g + 1) * group, fetch, 0)
+        for d in range(g * group, (g + 1) * group):
+            own = mix.at[pl.ds(d % 2 * 2 * first, 2 * first)]
+            fetch_rows(list_s, d, 0, (first,), src, own, (stage,))
         part = pl.ds(g * group, group)
         copies.append(pltpu.make_async_copy(stage.at[part], out.at[part], sem.at[g]))
         copies[-1].start()
@@ -168,23 +175,24 @@
         scratch_shapes=[
             pltpu.VMEM((devices, local), BF16),
             pltpu.VMEM((chunks * devices, 2 * LANES), F32),
-            pltpu.VMEM((4 * per, local), BF16),
+            pltpu.VMEM((3 * per, local), BF16),
             pltpu.VMEM((local, width), BF16),
             pltpu.VMEM((2 * (local + SUBLANES), LANES), F32),
+            pltpu.VMEM((4 * first, LANES), F32),
             pltpu.VMEM((devices, first + TAIL, width), BF16),
             pltpu.SMEM((devices, padded), jnp.int32),
-            pltpu.SemaphoreType.DMA((4,)),
+            pltpu.SemaphoreType.DMA((8,)),
         ],
         compiler_params=params(),
         name="send_first",
     )(placement.reshape(chunks, LANES), rows)
 
 
-def rest_kernel(list_ref, x_ref, one, two, src, *, first):
+def rest_kernel(list_ref, x_ref, one, two, src, mix, *, first):
     widen_rows(x_ref, src)
 
     def fetch(d, carry):
-        fetch_rows(list_ref, d, first, (one.shape[1], two.shape[1]), src, (one, two))
+        fetch_rows(list_ref, d, first, (one.shape[1], two.shape[1]), src, mix, (one, two))
         return carry
 
     lax.fori_loop(0, list_ref.shape[0], fetch, 0)
@@ -197,7 +205,10 @@
         functools.partial(rest_kernel, first=first),
         in_specs=[pl.BlockSpec(memory_space=pltpu.SMEM), pl.BlockSpec(memory_space=pltpu.VMEM)],
         out_shape=[jax.ShapeDtypeStruct((devices, n, width), BF16) for n in counts],
-        scratch_shapes=[pltpu.VMEM((2 * (local + SUBLANES), LANES), F32)],
+        scratch_shapes=[
+            pltpu.VMEM((2 * (local + SUBLANES), LANES), F32),
+            pltpu.VMEM((2 * sum(counts), LANES), F32),
+        ],
         compiler_params=params(),
         cost_estimate=pl.CostEstimate(
             flops=2_000_000 * devices * sum(counts), bytes_accessed=6_000_000, transcendentals=0

time: 152 us -> 150 us (0.987)
  Pallas kernels: 80.2 us -> 78.3 us
    pallas_call x1, Pallas kernels: 10.5 us -> 8.4 us  [send_first(): pl.pallas_call(functools.partial(send_kernel, groups=groups, shards=shard...]
where the time goes in v3:
time: 150 us; the launch traced here: 149 us
  Pallas kernels  78.3 us (52%)
  waiting for transfers between devices  37.9 us (25%)
  starting transfers between devices  27.8 us (19%)
  local copies, waits for them, and re-layouts  2.66 us (2%)
  other arithmetic  2.17 us (1%)
    pallas_call x3, Pallas kernels, finish_rows(): pl.pallas_call(functools.partial(finish_kernel, start=start, per=per, fol...  42.3 us
    ppermute x3, waiting for transfers between devices, sum_head(): lax.ppermute(value, 'head', [(i, i ^ k) for i in range(groups)])  25.8 us
    pallas_call x1, Pallas kernels, local_sums(): pl.pallas_call(sums_kernel, grid=(local // block,), in_specs=[pl.BlockSpe...  16 us
    all_to_all x3, starting transfers between devices, exchange(): lax.all_to_all(rows, ('head', 'pts'), split_axis=0, concat_axis=0, tiled=...  14 us
    pallas_call x1, Pallas kernels, send_first(): pl.pallas_call(functools.partial(send_kernel, groups=groups, shards=shard...  8.4 us
    all_to_all x3, waiting for transfers between devices, exchange(): lax.all_to_all(rows, ('head', 'pts'), split_axis=0, concat_axis=0, tiled=...  8.38 us
    pallas_call x1, Pallas kernels, send_rest(): pl.pallas_call(functools.partial(rest_kernel, first=first), in_specs=[pl....  7.41 us
    ppermute x3, starting transfers between devices, body(): lax.ppermute(softmax_sharpness, 'head', [(i, i ^ k) for i in range(groups)])  5.64 us
  transfers between devices with their start and end apart: 12, of which 6 were waited for; matrix products, arithmetic and copies ran while one was open for 3% of the time, Pallas kernels for 47%

profile of v3, /device:TPU:0, one launch (start us, length us, event | category | flops | bytes accessed | tf_op | source)
XLA Modules:
  0.0 149.1 jit_solution(8663342914043240677)
XLA Ops:
  0.0 4.1 %collective-permute-start.1 = (f32[4]{0:T(128)}, f32[4]{0:T(128)S(1)}, u32[]{:S(2)}, u32[]{:S(2)}) collective-permute-start(f32[4]{0:T(128)} %param.28), channel_id=1, source_target_pairs={{0,16},{8,24},{16,0},{24,8},{1,17},{9,25},{17,1},{25,9},{2,18},{10... | collective-permute-start | bytes 56 | tf_op jit(solution)/shard_map/ppermute | solution.py:551
  4.1 1.6 %collective-permute-start = (f32[4]{0:T(128)}, f32[4]{0:T(128)S(1)}, u32[]{:S(2)}, u32[]{:S(2)}) collective-permute-start(f32[4]{0:T(128)} %param.28), channel_id=1, source_target_pairs={{0,8},{8,0},{16,24},{24,16},{1,9},{9,1},{17,25},{25,17},{2,10},{10... | collective-permute-start | bytes 56 | tf_op jit(solution)/shard_map/ppermute | solution.py:551
  5.7 8.4 %send_first.1 = (s32[32,256]{1,0:T(8,128)}, bf16[32,104,256]{2,1,0:T(8,128)(2,1)}) custom-call(s32[48,128]{1,0:T(8,128)} %bitcast.17, bf16[6144,256]{1,0:T(8,128)(2,1)} %x_ref.3), custom_call_target="tpu_custom_call" | custom-call | tf_op jit(solution)/shard_map/send_first/pallas_call | solution.py:167
  14.1 6.1 %all-to-all-start = ((bf16[32,104,256]{2,1,0:T(8,128)(2,1)}), bf16[32,104,256]{2,1,0:T(8,128)(2,1)S(1)}, u32[]{:S(2)}, u32[]{:S(2)}) async-start(bf16[32,104,256]{2,1,0:T(8,128)(2,1)} %get-tuple-element.25), calls=%async_computation | async-start | bytes 3407872 | tf_op jit(solution)/shard_map/all_to_all | solution.py:548
  21.7 16.0 %local_sums.1 = (f32[32,384]{1,0:T(8,128)}, bf16[512,256]{1,0:T(8,128)(2,1)}) custom-call(bf16[6144,256]{1,0:T(8,128)(2,1)} %x_ref.3, f32[1,256]{1,0:T(1,128)} %bitcast.21, f32[1,256]{1,0:T(1,128)} %bitcast.25, bf16[256,256]{1,0:T(8,128)(2,1)} %attribute.1, bf16[256,256]{1,0:T(8,128)(2,1)} %bitcast.13, bf16[16,32]{1,0:T(8,128)(2,1)} %partition.1, ...), custom_call_target="tpu_custom_call" | custom-call | flops 5000000000 | bytes 4000000 | tf_op jit(solution)/shard_map/local_sums/pallas_call | solution.py:303
  38.0 1.2 collective-permute-done.3
  39.2 0.8 add.22
  40.0 1.8 %collective-permute-start.4 = (f32[32,384]{1,0:T(8,128)S(1)}, f32[32,384]{1,0:T(8,128)S(1)}, u32[]{:S(2)}, u32[]{:S(2)}) collective-permute-start(f32[32,384]{1,0:T(8,128)S(1)} %add.22), channel_id=1, source_target_pairs={{0,2},{1,3},{2,0},{3,1},{4,6},{5,7},{6,4},{7,5},{8,10},{9,11},{10,... | collective-permute-start | bytes 147464 | tf_op jit(solution)/shard_map/ppermute | solution.py:501
  41.8 2.5 %collective-permute-done.4 = f32[32,384]{1,0:T(8,128)S(1)} collective-permute-done((f32[32,384]{1,0:T(8,128)S(1)}, f32[32,384]{1,0:T(8,128)S(1)}, u32[]{:S(2)}, u32[]{:S(2)}) %collective-permute-start.4) | collective-permute-done | bytes 49184 | tf_op jit(solution)/shard_map/ppermute | solution.py:501
  44.3 1.7 %collective-permute-start.5 = (f32[32,384]{1,0:T(8,128)S(1)}, f32[32,384]{1,0:T(8,128)S(1)}, u32[]{:S(2)}, u32[]{:S(2)}) collective-permute-start(f32[32,384]{1,0:T(8,128)S(1)} %add.23), channel_id=1, source_target_pairs={{0,4},{1,5},{2,6},{3,7},{4,0},{5,1},{6,2},{7,3},{8,12},{9,13},{10,... | collective-permute-start | bytes 147464 | tf_op jit(solution)/shard_map/ppermute | solution.py:501
  45.9 7.4 %send_rest.1 = (bf16[32,64,256]{2,1,0:T(8,128)(2,1)}, bf16[32,32,256]{2,1,0:T(8,128)(2,1)}) custom-call(s32[32,256]{1,0:T(8,128)} %get-tuple-element.26.list_ref, bf16[6144,256]{1,0:T(8,128)(2,1)} %x_ref.3), custom_call_target="tpu_custom_call" | custom-call | flops 6144000000 | bytes 6000000 | tf_op jit(solution)/shard_map/send_rest/pallas_call | solution.py:204
  53.4 7.2 %all-to-all-done.x_ref = bf16[32,104,256]{2,1,0:T(8,128)(2,1)S(1)} async-done(((bf16[32,104,256]{2,1,0:T(8,128)(2,1)}), bf16[32,104,256]{2,1,0:T(8,128)(2,1)S(1)}, u32[]{:S(2)}, u32[]{:S(2)}) %all-to-all-start) | async-done | bytes 1703968 | tf_op jit(solution)/shard_map/all_to_all | solution.py:548
  60.6 4.1 %all-to-all-start.1 = ((bf16[32,64,256]{2,1,0:T(8,128)(2,1)}), bf16[32,64,256]{2,1,0:T(8,128)(2,1)S(1)}, u32[]{:S(2)}, u32[]{:S(2)}) async-start(bf16[32,64,256]{2,1,0:T(8,128)(2,1)} %get-tuple-element.30), calls=%async_computation.1 | async-start | bytes 2097152 | tf_op jit(solution)/shard_map/all_to_all | solution.py:548
  64.7 3.5 %collective-permute-start.8 = (f32[32,384]{1,0:T(8,128)S(1)}, f32[32,384]{1,0:T(8,128)S(1)}, u32[]{:S(2)}, u32[]{:S(2)}) collective-permute-start(f32[32,384]{1,0:T(8,128)S(1)} %add.24), channel_id=1, source_target_pairs={{0,24},{8,16},{16,8},{24,0},{1,25},{9,17},{17,9},{25,1},{2,26},{10... | collective-permute-start | bytes 147464 | tf_op jit(solution)/shard_map/ppermute | solution.py:507
  68.2 0.9 collective-permute-start.6
  69.2 18.5 %collective-permute-done.8 = f32[32,384]{1,0:T(8,128)S(1)} collective-permute-done((f32[32,384]{1,0:T(8,128)S(1)}, f32[32,384]{1,0:T(8,128)S(1)}, u32[]{:S(2)}, u32[]{:S(2)}) %collective-permute-start.8) | collective-permute-done | bytes 49184 | tf_op jit(solution)/shard_map/ppermute | solution.py:507
  87.7 7.3 %collective-permute-done.7 = f32[32,384]{1,0:T(8,128)S(1)} collective-permute-done((f32[32,384]{1,0:T(8,128)S(1)}, f32[32,384]{1,0:T(8,128)S(1)}, u32[]{:S(2)}, u32[]{:S(2)}) %collective-permute-start.7) | collective-permute-done | bytes 49184 | tf_op jit(solution)/shard_map/ppermute | solution.py:507
  95.6 4.2 %slice_attention.1.mix_t = bf16[256,512]{1,0:T(8,128)(2,1)} custom-call(f32[32,384]{1,0:T(8,128)} %add_add_fusion.packed_ref, f32[16,16]{1,0:T(8,128)} %question.1, f32[16,16]{1,0:T(8,128)} %lookup.1, f32[16,16]{1,0:T(8,128)} %content.1), custom_call_target="tpu_custom_call" | custom-call | tf_op jit(solution)/shard_map/slice_attention/pallas_call | solution.py:368
  100.8 19.6 %shard_map.190.refs_0_ = f32[12288,128]{1,0:T(8,128)} custom-call(s32[32,256]{1,0:T(8,128)} %fusion.1.pos_hbm, bf16[32,104,256]{2,1,0:T(8,128)(2,1)} %copy-done, f32[1,256]{1,0:T(1,128)} %bitcast.22, f32[1,256]{1,0:T(1,128)} %bitcast.26, bf16[256,256]{1,0:T(8,128)(2,1)} %bitcast.14, bf16[512,256]{1,0:T(8,128)(2,1)} %get-tuple-element.29.logit_t, ...), custom_call_target="tpu_custom_call" | custom-call | flops 6144000000 | bytes 8000000 | tf_op jit(solution)/shard_map/pallas_call | solution.py:467
  120.4 3.9 %all-to-all-start.2 = ((bf16[32,32,256]{2,1,0:T(8,128)(2,1)}), bf16[32,32,256]{2,1,0:T(8,128)(2,1)S(1)}, u32[]{:S(2)}, u32[]{:S(2)}) async-start(bf16[32,32,256]{2,1,0:T(8,128)(2,1)} %get-tuple-element.32), calls=%async_computation.2 | async-start | bytes 1048576 | tf_op jit(solution)/shard_map/all_to_all | solution.py:548
  124.3 14.2 %shard_map.191.refs_0_ = f32[12288,128]{1,0:T(8,128)} custom-call(s32[32,256]{1,0:T(8,128)} %fusion.1.pos_hbm, bf16[32,64,256]{2,1,0:T(8,128)(2,1)} %copy-done.1, f32[1,256]{1,0:T(1,128)} %bitcast.23, f32[1,256]{1,0:T(1,128)} %bitcast.27, bf16[256,256]{1,0:T(8,128)(2,1)} %bitcast.15, bf16[512,256]{1,0:T(8,128)(2,1)} %get-tuple-element.29.logit_t, ...), custom_call_target="tpu_custom_call" | custom-call | flops 4096000000 | bytes 8000000 | tf_op jit(solution)/shard_map/pallas_call | solution.py:467
  138.5 1.1 all-to-all-done.2.x_ref
  139.7 0.8 copy-done.2
  140.5 8.5 %shard_map.192 = bf16[6144,256]{1,0:T(8,128)(2,1)} custom-call(s32[32,256]{1,0:T(8,128)} %fusion.1.pos_hbm, bf16[32,32,256]{2,1,0:T(8,128)(2,1)} %copy-done.2, f32[1,256]{1,0:T(1,128)} %bitcast.24, f32[1,256]{1,0:T(1,128)} %bitcast.28, bf16[256,256]{1,0:T(8,128)(2,1)} %bitcast.16, bf16[512,256]{1,0:T(8,128)(2,1)} %get-tuple-element.29.logit_t, ...), custom_call_target="tpu_custom_call" | custom-call | flops 2048000000 | bytes 8000000 | tf_op jit(solution)/shard_map/pallas_call | solution.py:467
  (30 shorter events, 3.5 us)
Async XLA Ops:
  0.0 14.1 %collective-permute-start.1 = (f32[4]{0:T(128)}, f32[4]{0:T(128)S(1)}, u32[]{:S(2)}, u32[]{:S(2)}) collective-permute-start(f32[4]{0:T(128)} %param.28), channel_id=1, source_target_pairs={{0,16},{8,24},{16,0},{24,8},{1,17},{9,25},{17,1},{25,9},{2,18},{10... | collective-permute-start | bytes 56 | tf_op jit(solution)/shard_map/ppermute | solution.py:551
  4.1 10.0 %collective-permute-start = (f32[4]{0:T(128)}, f32[4]{0:T(128)S(1)}, u32[]{:S(2)}, u32[]{:S(2)}) collective-permute-start(f32[4]{0:T(128)} %param.28), channel_id=1, source_target_pairs={{0,8},{8,0},{16,24},{24,16},{1,9},{9,1},{17,25},{25,17},{2,10},{10... | collective-permute-start | bytes 56 | tf_op jit(solution)/shard_map/ppermute | solution.py:551
  5.6 8.4 %collective-permute-start.2 = (f32[4]{0:T(128)}, f32[4]{0:T(128)S(1)}, u32[]{:S(2)}, u32[]{:S(2)}) collective-permute-start(f32[4]{0:T(128)} %param.28), channel_id=1, source_target_pairs={{0,24},{8,16},{16,8},{24,0},{1,25},{9,17},{17,9},{25,1},{2,26},{10... | collective-permute-start | bytes 56 | tf_op jit(solution)/shard_map/ppermute | solution.py:551
  5.6 14.5 %copy-start.3 = (bf16[256,256]{1,0:T(8,128)(2,1)S(1)}, bf16[256,256]{1,0:T(8,128)(2,1)}, u32[]{:S(2)}) copy-start(bf16[256,256]{1,0:T(8,128)(2,1)} %param.25) | copy-start | bytes 393220
  5.6 15.3 %copy-start.4 = (f32[4]{0:T(128)S(1)}, f32[4]{0:T(128)}, u32[]{:S(2)}) copy-start(f32[4]{0:T(128)} %param.28) | copy-start | bytes 52
  14.1 46.5 %all-to-all-start = ((bf16[32,104,256]{2,1,0:T(8,128)(2,1)}), bf16[32,104,256]{2,1,0:T(8,128)(2,1)S(1)}, u32[]{:S(2)}, u32[]{:S(2)}) async-start(bf16[32,104,256]{2,1,0:T(8,128)(2,1)} %get-tuple-element.25), calls=%async_computation | async-start | bytes 3407872 | tf_op jit(solution)/shard_map/all_to_all | solution.py:548
  37.7 1.4 collective-permute-start.3
  40.0 4.3 %collective-permute-start.4 = (f32[32,384]{1,0:T(8,128)S(1)}, f32[32,384]{1,0:T(8,128)S(1)}, u32[]{:S(2)}, u32[]{:S(2)}) collective-permute-start(f32[32,384]{1,0:T(8,128)S(1)} %add.22), channel_id=1, source_target_pairs={{0,2},{1,3},{2,0},{3,1},{4,6},{5,7},{6,4},{7,5},{8,10},{9,11},{10,... | collective-permute-start | bytes 147464 | tf_op jit(solution)/shard_map/ppermute | solution.py:501
  44.3 9.1 %collective-permute-start.5 = (f32[32,384]{1,0:T(8,128)S(1)}, f32[32,384]{1,0:T(8,128)S(1)}, u32[]{:S(2)}, u32[]{:S(2)}) collective-permute-start(f32[32,384]{1,0:T(8,128)S(1)} %add.23), channel_id=1, source_target_pairs={{0,4},{1,5},{2,6},{3,7},{4,0},{5,1},{6,2},{7,3},{8,12},{9,13},{10,... | collective-permute-start | bytes 147464 | tf_op jit(solution)/shard_map/ppermute | solution.py:501
  60.6 39.6 %copy-start = (bf16[32,104,256]{2,1,0:T(8,128)(2,1)}, bf16[32,104,256]{2,1,0:T(8,128)(2,1)S(1)}, u32[]{:S(2)}) copy-start(bf16[32,104,256]{2,1,0:T(8,128)(2,1)S(1)} %all-to-all-done.x_ref) | copy-start | bytes 5111812
  60.6 59.8 %all-to-all-start.1 = ((bf16[32,64,256]{2,1,0:T(8,128)(2,1)}), bf16[32,64,256]{2,1,0:T(8,128)(2,1)S(1)}, u32[]{:S(2)}, u32[]{:S(2)}) async-start(bf16[32,64,256]{2,1,0:T(8,128)(2,1)} %get-tuple-element.30), calls=%async_computation.1 | async-start | bytes 2097152 | tf_op jit(solution)/shard_map/all_to_all | solution.py:548
  64.7 23.0 %collective-permute-start.8 = (f32[32,384]{1,0:T(8,128)S(1)}, f32[32,384]{1,0:T(8,128)S(1)}, u32[]{:S(2)}, u32[]{:S(2)}) collective-permute-start(f32[32,384]{1,0:T(8,128)S(1)} %add.24), channel_id=1, source_target_pairs={{0,24},{8,16},{16,8},{24,0},{1,25},{9,17},{17,9},{25,1},{2,26},{10... | collective-permute-start | bytes 147464 | tf_op jit(solution)/shard_map/ppermute | solution.py:507
  68.2 26.7 %collective-permute-start.7 = (f32[32,384]{1,0:T(8,128)S(1)}, f32[32,384]{1,0:T(8,128)S(1)}, u32[]{:S(2)}, u32[]{:S(2)}) collective-permute-start(f32[32,384]{1,0:T(8,128)S(1)} %add.24), channel_id=1, source_target_pairs={{0,16},{8,24},{16,0},{24,8},{1,17},{9,25},{17,1},{25,9},{2,18},{10... | collective-permute-start | bytes 147464 | tf_op jit(solution)/shard_map/ppermute | solution.py:507
  68.2 26.7 %collective-permute-start.6 = (f32[32,384]{1,0:T(8,128)S(1)}, f32[32,384]{1,0:T(8,128)S(1)}, u32[]{:S(2)}, u32[]{:S(2)}) collective-permute-start(f32[32,384]{1,0:T(8,128)S(1)} %add.24), channel_id=1, source_target_pairs={{0,8},{8,0},{16,24},{24,16},{1,9},{9,1},{17,25},{25,17},{2,10},{10... | collective-permute-start | bytes 147464 | tf_op jit(solution)/shard_map/ppermute | solution.py:507
  120.4 3.9 %copy-start.1 = (bf16[32,64,256]{2,1,0:T(8,128)(2,1)}, bf16[32,64,256]{2,1,0:T(8,128)(2,1)S(1)}, u32[]{:S(2)}) copy-start(bf16[32,64,256]{2,1,0:T(8,128)(2,1)S(1)} %all-to-all-done.1.x_ref) | copy-start | bytes 3145732
  120.4 19.3 %all-to-all-start.2 = ((bf16[32,32,256]{2,1,0:T(8,128)(2,1)}), bf16[32,32,256]{2,1,0:T(8,128)(2,1)S(1)}, u32[]{:S(2)}, u32[]{:S(2)}) async-start(bf16[32,32,256]{2,1,0:T(8,128)(2,1)} %get-tuple-element.32), calls=%async_computation.2 | async-start | bytes 1048576 | tf_op jit(solution)/shard_map/all_to_all | solution.py:548
  139.7 0.8 copy-start.2
